TPU v7x, 256 devices: a 4x2x16 block of a 4x16x16 slice. The times are simulated.
256 devices in a mesh: grp: 2 (over y), col: 32 (over z, core), blk: 4 (over x).
Axes of the slice: x: 4, y: 2, z: 16, core: 2. Of those that a mesh axis runs over, the one named last changes fastest.
The devices are a block of a 4x16x16 slice.
Arguments:
- boundary: bfloat16 [256, 192, 576], P(('grp', 'col'), 'blk'), parts along dimension 0, may hold values from -6 to 6
- row_tensor: bfloat16 [256, 6, 6, 6, 6], P(('grp', 'col')), parts along dimension 0, may hold values from -1.5 to 1.5
- left_proj: bfloat16 [256, 192, 576], P(('grp', 'col'), 'blk'), parts along dimension 0, may hold values from -0.75 to 0.75
- right_proj: bfloat16 [256, 192, 576], P(('grp', 'col'), 'blk'), parts along dimension 0, may hold values from -0.3125 to 0.3125
- leg_parity: int32 [256, 3, 6], P('grp'), parts along dimension 0, may hold values from 0 to 1
- bond_charges: int32 [256, 2], P('grp'), parts along dimension 0, may hold values from 32 to 96, as said below
Outputs:
- new_boundary: bfloat16 [256, 192, 576], P(('grp', 'col'), 'blk'), parts along dimension 0
There are 2 independent parts, one for each index of `grp`. A program takes and returns all parts, laid end to end along the dimension named above; each array names one. Nothing has to cross between parts.
Inputs may be any that keep to these rules, and one draw needn't show every extreme that they name: `bond_charges`: odd counts are 128 minus these, so neither block of a bond holds more than 96 live rows; some bond has an even count of 96 and some bond an odd count of 96. `leg_parity`: [c, 0] is the horizontal leg left of column c, [c, 1] the vertical leg between boundary and row, [c, 2] the outgoing vertical leg.
All inputs are finite; a program needn't handle non-finite values.
Results may differ from a plain program's by a relative error of at most 0.0057.
Values may be sent and summed in bfloat16 or wider, within the bound.
No kernel may reach another device: no remote copies, remote signals or barrier semaphores. Data moves between devices by JAX's collectives and lax.ppermute only.
A program may use at most 64 MiB of HBM per device.

v0:
```python
import jax
import jax.numpy as jnp
from jax import lax
from jax.sharding import PartitionSpec as P

CHI = 128
BLOCK = 96
D = 6


def from_everyone(x, axis):
    length = lax.axis_size(axis)
    return lax.all_to_all(jnp.broadcast_to(x[None], (length, *x.shape)), axis, 0, 0, tiled=True)


def joined_along(pieces, dim):
    dims = list(pieces.shape[1:])
    dims[dim] *= pieces.shape[0]
    return jnp.moveaxis(pieces, 0, dim).reshape(dims)


def gathered_copies(x, axis, dim):
    pieces = from_everyone(x, axis)
    return joined_along(pieces, dim)


def passed_along(x, axis, by):
    length = lax.axis_size(axis)
    return lax.ppermute(x, axis, [(i, (i + by) % length) for i in range(length)])


def live_rows(counts, parity, position):
    limit = jnp.where(parity == 0, counts, CHI - counts)
    return position < limit


def per_device(boundary, row_tensor, left_proj, right_proj, leg_parity, bond_charges):
    col_dev, sub_rows, merged = boundary.shape
    start_col = lax.axis_index("col") * col_dev
    charges_here = lax.dynamic_slice_in_dim(bond_charges, start_col, col_dev, 0)
    charges_next = lax.dynamic_slice_in_dim(jnp.roll(bond_charges, -1, 0), start_col, col_dev, 0)
    legs_here = lax.dynamic_slice_in_dim(leg_parity, start_col, col_dev, 0)
    legs_next = lax.dynamic_slice_in_dim(jnp.roll(leg_parity, -1, 0), start_col, col_dev, 0)
    in_here = charges_here[:, 0]
    out_here = charges_here[:, 1]
    in_next = charges_next[:, 0]
    out_next = charges_next[:, 1]
    left_leg = legs_here[:, 0]
    up_leg = legs_here[:, 1]
    down_leg = legs_here[:, 2]
    right_leg = legs_next[:, 0]
    inside = lax.iota(jnp.int32, BLOCK)
    row_start = lax.axis_index("blk") * sub_rows
    local_index = row_start + lax.iota(jnp.int32, sub_rows)
    local_parity = local_index // BLOCK
    local_position = local_index % BLOCK
    left_sel = (local_parity[None, :, None] + left_leg[:, None, :]) % 2
    left_mask = live_rows(out_here[:, None], local_parity[None, :], local_position[None, :])[
        :, :, None, None
    ] & live_rows(in_here[:, None, None, None], left_sel[..., None], inside[None, None, None, :])
    left_m = left_proj.reshape(col_dev, sub_rows, D, BLOCK) * left_mask.astype(jnp.bfloat16)
    left_dense = jnp.concatenate(
        [
            left_m * (left_sel == 0).astype(jnp.bfloat16)[..., None],
            left_m * (left_sel == 1).astype(jnp.bfloat16)[..., None],
        ],
        axis=3,
    )
    piece = gathered_copies(boundary, "blk", 1)
    count_rows = piece.shape[1]
    row_index = lax.iota(jnp.int32, count_rows)
    row_parity = row_index // BLOCK
    row_position = row_index % BLOCK
    bound_sel = (row_parity[None, :, None] + up_leg[:, None, :]) % 2
    bound_mask = live_rows(in_here[:, None], row_parity[None, :], row_position[None, :])[
        :, :, None, None
    ] & live_rows(in_next[:, None, None, None], bound_sel[..., None], inside[None, None, None, :])
    piece_m = piece.reshape(col_dev, count_rows, D, BLOCK) * bound_mask.astype(jnp.bfloat16)
    absorbed = jnp.einsum(
        "cpla,caub->cplub", left_dense, piece_m, preferred_element_type=jnp.float32
    ).astype(jnp.bfloat16)
    row_keep = (
        left_leg[:, :, None, None, None]
        + up_leg[:, None, :, None, None]
        + down_leg[:, None, None, :, None]
        + right_leg[:, None, None, None, :]
    ) % 2 == 0
    row_sign = 1 - 2 * left_leg[:, :, None, None, None] * up_leg[:, None, :, None, None]
    row_m = row_tensor * jnp.where(row_keep, row_sign, 0).astype(jnp.bfloat16)
    mixed = jnp.einsum("cplub,cludr->cpdrb", absorbed, row_m, preferred_element_type=jnp.float32)
    block_par = (
        local_parity[None, :, None, None] + down_leg[:, None, :, None] + right_leg[:, None, None, :]
    ) % 2
    sign_flip = (1 - 2 * block_par * down_leg[:, None, :, None]).astype(jnp.float32)
    mixed = (mixed * sign_flip[..., None]).astype(jnp.bfloat16)
    mixed_dense = jnp.concatenate(
        [
            mixed * (block_par == 0).astype(jnp.bfloat16)[..., None],
            mixed * (block_par == 1).astype(jnp.bfloat16)[..., None],
        ],
        axis=4,
    )
    incoming = passed_along(right_proj[:1], "col", -1)
    right_next = jnp.concatenate([right_proj[1:], incoming], axis=0)
    piece = gathered_copies(right_next, "blk", 1)
    count_rows = piece.shape[1]
    row_index = lax.iota(jnp.int32, count_rows)
    row_parity = row_index // BLOCK
    row_position = row_index % BLOCK
    right_sel = (row_parity[None, :, None] + right_leg[:, None, :]) % 2
    right_mask = live_rows(in_next[:, None], row_parity[None, :], row_position[None, :])[
        :, :, None, None
    ] & live_rows(out_next[:, None, None, None], right_sel[..., None], inside[None, None, None, :])
    piece_m = piece.reshape(col_dev, count_rows, D, BLOCK) * right_mask.astype(jnp.bfloat16)
    result = jnp.einsum(
        "cpdrb,cbre->cpde", mixed_dense, piece_m, preferred_element_type=jnp.float32
    )
    return result.astype(jnp.bfloat16).reshape(col_dev, sub_rows, merged)


def solution(mesh):
    in_specs = (
        P(("grp", "col"), "blk", None),
        P(("grp", "col"), None, None, None, None),
        P(("grp", "col"), "blk", None),
        P(("grp", "col"), "blk", None),
        P("grp", None, None),
        P("grp", None),
    )
    out_specs = P(("grp", "col"), "blk", None)
    return jax.shard_map(
        per_device, mesh=mesh, in_specs=in_specs, out_specs=out_specs, check_vma=False
    )
```

profile of v0, /device:TPU:40, one launch (start us, length us, event | category | flops | bytes accessed | tf_op | source)
XLA Modules:
  0.0 71.8 jit_solution(1000798347300259663)
XLA Ops:
  0.0 0.0 copy-start.2
  0.0 0.0 copy-start.6
  0.0 2.0 %broadcast_in_dim.170 = bf16[4,4,48,576]{3,2,1,0:T(8,128)(2,1)} broadcast(bf16[4,48,576]{2,1,0:T(8,128)(2,1)} %param.6), dimensions={1,2,3} | broadcast | bytes 1105920 | tf_op jit(solution)/shard_map/broadcast_in_dim | solution.py:13
  2.1 4.6 %all-to-all-start = ((bf16[4,4,48,576]{3,2,1,0:T(8,128)(2,1)}), bf16[4,4,48,576]{3,2,1,0:T(8,128)(2,1)S(1)}, u32[]{:S(2)}, u32[]{:S(2)}) async-start(bf16[4,4,48,576]{3,2,1,0:T(8,128)(2,1)} %broadcast_in_dim.170), calls=%async_computation | async-start | bytes 1966080 | tf_op jit(solution)/shard_map/all_to_all | solution.py:13
  6.6 0.0 copy-done.2
  6.7 21.7 %collective-permute-start = (bf16[1,48,576]{2,1,0:T(8,128)(2,1)S(1)}, bf16[1,48,576]{2,1,0:T(8,128)(2,1)S(1)}, u32[]{:S(2)}, u32[]{:S(2)}) collective-permute-start(bf16[1,48,576]{2,1,0:T(8,128)(2,1)S(1)} %slice.62), channel_id=1, source_target_pairs={{0,124},{4,0},{8,4},{12,8},{16,12},{20,16},{24,20},{28,24},{32,28}... | collective-permute-start | bytes 165896 | tf_op jit(solution)/shard_map/ppermute | solution.py:29
  28.3 0.0 copy-done.10
  28.3 0.1 slice.57
  28.4 0.1 pad_add_fusion
  28.5 0.1 constant_dynamic-slice_fusion.2
  28.6 0.0 copy-done.9
  28.7 0.1 slice.51
  28.7 0.1 constant_dynamic-slice_fusion.1
  28.8 0.1 copy.39
  28.9 0.1 copy.35
  29.0 0.1 copy.33
  29.1 0.1 copy.37
  29.2 0.1 copy.34
  29.3 0.1 fusion.39
  29.4 0.0 copy-done.6
  29.4 0.0 slice-start
  29.4 0.3 reshape.405
  29.7 0.1 copy.40
  29.8 0.1 copy.36
  29.9 0.1 copy.38
  30.0 0.1 broadcast_select_fusion
  30.1 1.2 %compare_convert_fusion.1 = (bf16[4,48,6,6]{3,1,2,0:T(8,128)(2,1)}, bf16[4,48,6,6]{3,1,2,0:T(8,128)(2,1)}) fusion(s32[4,6]{1,0:T(4,128)S(1)} %bitcast.62, s32[4,48,6]{1,2,0:T(8,128)S(1)} %get-tuple-element.32), kind=kLoop, calls=%fused_computation.51 | loop fusion | flops 110592 | bytes 32352 | tf_op jit(solution)/shard_map/convert_element_type | solution.py:98
  31.3 1.2 %subtract_convert_fusion = f32[4,48,6,6]{3,1,2,0:T(8,128)} fusion(s32[4,6]{1,0:T(4,128)S(1)} %broadcast_multiply_fusion.4, s32[4,6]{1,0:T(4,128)S(1)} %bitcast.63, s32[4,48,6]{1,2,0:T(8,128)S(1)} %get-tuple-element.32), kind=kLoop, calls=%fused_computation.46 | loop fusion | flops 103680 | bytes 32448 | tf_op jit(solution)/shard_map/convert_element_type | solution.py:94
  32.5 0.1 select_compare_fusion.2
  32.6 1.3 %fusion.32 = (s32[4,192,6]{2,1,0:T(8,128)}, s32[4,192,6]{2,1,0:T(8,128)}) fusion(s32[4]{0:T(128)S(1)} %get-tuple-element.25, s32[4]{0:T(128)S(1)} %get-tuple-element.21, s32[4,6]{1,0:T(4,128)S(1)} %bitcast.64, s32[192]{0:T(256)S(1)} %get-tuple-element.33, s32[4]{0:T(128)S(1)} %get-tuple-element.26, s32[4]{0:T(128)S(1)} %get-tuple-element.22, ...), kind=kLoop, calls=%fused_computation.59 | loop fusion | flops 129024 | bytes 37888 | tf_op jit(solution)/shard_map/jit(_where)/select_n | solution.py:33
  33.9 1.4 %broadcast_multiply_fusion.3 = (bf16[4,48,6,96]{3,1,2,0:T(8,128)(2,1)}, bf16[4,48,6,96]{3,1,2,0:T(8,128)(2,1)}) fusion(bf16[4,48,6]{1,2,0:T(8,128)(2,1)S(1)} %get-tuple-element.16, bf16[4,48,6,96]{3,2,1,0:T(8,128)(2,1)S(1)} %reshape.405, s32[4,48,6]{1,2,0:T(8,128)S(1)} %get-tuple-element.31, pred[4,48]{1,0:T(4,128)(4,1)S(1)} %select_compare_fusion.2, ...), kind=kLoop, calls=%fused_computation.66 | loop fusion | flops 1105920 | bytes 672960 | tf_op jit(solution)/shard_map/mul | solution.py:64
  35.3 0.0 copy-done.7
  35.3 1.3 %fusion.36 = bf16[4,6,6,6,6,1]{4,0,3,2,1,5:T(4,128)(2,1)} fusion(bf16[4,6,6,6,6]{4,0,3,2,1:T(4,128)(2,1)S(1)} %copy-done.7, s32[4,6,6]{0,2,1:T(8,128)S(1)} %get-tuple-element.15, s32[4,6]{1,0:T(4,128)S(1)} %bitcast.65, s32[4,6,6,6]{0,3,2,1:T(8,128)S(1)} %broadcast_add_fusion), kind=kLoop, calls=%fused_computation.64 | loop fusion | flops 98496 | bytes 24864 | tf_op jit(solution)/shard_map/mul | solution.py:89
  36.6 0.1 select_compare_fusion
  36.7 0.0 collective-permute-done
  36.7 0.0 slice-done
  36.7 0.0 all-to-all-done
  36.7 1.1 %broadcast_in_dim.176 = bf16[4,4,48,576]{3,2,1,0:T(8,128)(2,1)} broadcast(bf16[4,48,576]{2,1,0:T(8,128)(2,1)S(1)} %pad_maximum_fusion.1), dimensions={1,2,3} | broadcast | bytes 1105920 | tf_op jit(solution)/shard_map/broadcast_in_dim | solution.py:13
  37.8 4.5 %all-to-all-start.1 = ((bf16[4,4,48,576]{3,2,1,0:T(8,128)(2,1)}), bf16[4,4,48,576]{3,2,1,0:T(8,128)(2,1)S(1)}, u32[]{:S(2)}, u32[]{:S(2)}) async-start(bf16[4,4,48,576]{3,2,1,0:T(8,128)(2,1)} %broadcast_in_dim.176), calls=%async_computation.1 | async-start | bytes 1966080 | tf_op jit(solution)/shard_map/all_to_all | solution.py:13
  42.3 0.1 copy.42
  42.4 1.2 %reshape_reshape.6 = bf16[4,192,6,96]{3,2,1,0:T(8,128)(2,1)S(1)} reshape(bf16[4,4,48,576]{3,2,1,0:T(8,128)(2,1)S(1)} %copy.42) | data formatting | bytes 1769472 | tf_op jit(solution)/shard_map/reshape;reshape | solution.py:78
  43.7 0.0 copy-start
  43.7 0.0 copy-start.1
  43.7 4.8 %fusion.12 = bf16[4,192,6,96,1]{3,2,1,0,4:T(8,128)(2,1)S(1)} fusion(bf16[4,192,6,96]{3,2,1,0:T(8,128)(2,1)S(1)} %reshape_reshape.6, s32[4,192,6]{2,1,0:T(8,128)} %get-tuple-element.24, pred[4,192]{1,0:T(4,128)(4,1)S(1)} %get-tuple-element.19), kind=kLoop, calls=%fused_computation.15 | loop fusion | flops 1327104 | bytes 1788672 | tf_op jit(solution)/shard_map/mul | solution.py:78
  48.5 0.0 copy-start.3
  48.5 0.0 copy-start.4
  48.5 0.0 copy-start.5
  48.5 0.0 copy-start.8
  48.5 0.0 copy-done
  48.6 0.0 copy-done.1
  48.6 0.7 convert_bitcast_fusion
  49.2 0.3 copy-done.3
  49.6 0.1 copy-done.4
  49.6 0.1 copy-done.5
  49.7 0.1 copy-done.8
  49.8 6.6 %broadcast_multiply_fusion.1 = (bf16[4,48,6,6,96]{4,3,1,2,0:T(8,128)(2,1)S(1)}, bf16[4,48,6,6,96]{4,3,1,2,0:T(8,128)(2,1)S(1)}) fusion(bf16[4,48,6,6]{3,1,2,0:T(8,128)(2,1)S(1)} %copy-done.4, bf16[4,48,6,6]{3,1,2,0:T(8,128)(2,1)S(1)} %copy-done.5, f32[4,48,6,6]{3,1,2,0:T(8,128)S(1)} %copy-done.3, ...), kind=kOutput, calls=%fused_computation.21 | convolution fusion | flops 50429952 | bytes 4046976 | tf_op jit(solution)/shard_map/cplub,cludr->cpdrb/dot_general | solution.py:90
  56.4 4.5 %pad_maximum_fusion = bf16[4,48,6,6,192]{4,3,1,2,0:T(8,128)(2,1)} fusion(bf16[4,48,6,6,96]{4,3,1,2,0:T(8,128)(2,1)S(1)} %get-tuple-element.6, bf16[4,48,6,6,96]{4,3,1,2,0:T(8,128)(2,1)S(1)} %get-tuple-element.5), kind=kLoop, calls=%fused_computation | loop fusion | flops 5308416 | bytes 5308416 | tf_op jit(solution)/shard_map/concatenate | solution.py:96
  60.9 0.0 all-to-all-done.1
  60.9 0.1 copy.46
  61.0 1.2 %reshape_reshape.7 = bf16[4,192,6,96]{3,2,1,0:T(8,128)(2,1)S(1)} reshape(bf16[4,4,48,576]{3,2,1,0:T(8,128)(2,1)S(1)} %copy.46) | data formatting | bytes 1769472 | tf_op jit(solution)/shard_map/reshape;reshape | solution.py:114
  62.2 4.7 %fusion.11 = bf16[4,192,6,96,1]{3,2,1,0,4:T(8,128)(2,1)S(1)} fusion(bf16[4,192,6,96]{3,2,1,0:T(8,128)(2,1)S(1)} %reshape_reshape.7, s32[4,192,6]{2,1,0:T(8,128)} %get-tuple-element.23, pred[4,192]{1,0:T(4,128)(4,1)S(1)} %get-tuple-element.18), kind=kLoop, calls=%fused_computation.14 | loop fusion | flops 1327104 | bytes 1788672 | tf_op jit(solution)/shard_map/mul | solution.py:114
  67.0 3.7 %fusion.16 = bf16[4,48,6,96]{3,1,2,0:T(8,128)(2,1)S(1)} fusion(bf16[4,48,6,6,192]{4,3,1,2,0:T(8,128)(2,1)} %pad_maximum_fusion, bf16[4,192,6,96,1]{3,2,1,0,4:T(8,128)(2,1)S(1)} %fusion.11), kind=kOutput, calls=%fused_computation.17 | convolution fusion | flops 254914560 | bytes 3760128 | tf_op jit(solution)/shard_map/cpdrb,cbre->cpde/dot_general | solution.py:115
  70.7 0.1 copy.49
  70.8 1.0 %reshape.406 = bf16[4,48,576]{2,1,0:T(8,128)(2,1)} reshape(bf16[4,48,6,96]{3,2,1,0:T(8,128)(2,1)S(1)} %copy.49) | data formatting | bytes 442368 | tf_op jit(solution)/shard_map/reshape | solution.py:118
  (17 shorter events, 0.1 us)
Async XLA Ops:
  0.0 6.6 %copy-start.2 = (bf16[4,48,576]{2,1,0:T(8,128)(2,1)S(1)}, bf16[4,48,576]{2,1,0:T(8,128)(2,1)}, u32[]{:S(2)}) copy-start(bf16[4,48,576]{2,1,0:T(8,128)(2,1)} %param.9) | copy-start | bytes 663556
  0.0 28.3 %copy-start.10 = (s32[128,2]{0,1:T(2,128)S(1)}, s32[128,2]{0,1:T(2,128)}, u32[]{:S(2)}) copy-start(s32[128,2]{0,1:T(2,128)} %param.11) | copy-start | bytes 3076
  0.0 28.6 %copy-start.9 = (s32[128,3,6]{0,2,1:T(8,128)S(1)}, s32[128,3,6]{0,2,1:T(8,128)}, u32[]{:S(2)}) copy-start(s32[128,3,6]{0,2,1:T(8,128)} %param.10) | copy-start | bytes 27652
  0.0 29.4 %copy-start.6 = (bf16[4,48,576]{2,1,0:T(8,128)(2,1)S(1)}, bf16[4,48,576]{2,1,0:T(8,128)(2,1)}, u32[]{:S(2)}) copy-start(bf16[4,48,576]{2,1,0:T(8,128)(2,1)} %param.8) | copy-start | bytes 663556
  2.1 34.7 %all-to-all-start = ((bf16[4,4,48,576]{3,2,1,0:T(8,128)(2,1)}), bf16[4,4,48,576]{3,2,1,0:T(8,128)(2,1)S(1)}, u32[]{:S(2)}, u32[]{:S(2)}) async-start(bf16[4,4,48,576]{3,2,1,0:T(8,128)(2,1)} %broadcast_in_dim.170), calls=%async_computation | async-start | bytes 1966080 | tf_op jit(solution)/shard_map/all_to_all | solution.py:13
  6.7 28.6 %copy-start.7 = (bf16[4,6,6,6,6]{4,0,3,2,1:T(4,128)(2,1)S(1)}, bf16[4,6,6,6,6]{4,0,3,2,1:T(4,128)(2,1)}, u32[]{:S(2)}) copy-start(bf16[4,6,6,6,6]{4,0,3,2,1:T(4,128)(2,1)} %param.7) | copy-start | bytes 31108
  6.7 30.0 %collective-permute-start = (bf16[1,48,576]{2,1,0:T(8,128)(2,1)S(1)}, bf16[1,48,576]{2,1,0:T(8,128)(2,1)S(1)}, u32[]{:S(2)}, u32[]{:S(2)}) collective-permute-start(bf16[1,48,576]{2,1,0:T(8,128)(2,1)S(1)} %slice.62), channel_id=1, source_target_pairs={{0,124},{4,0},{8,4},{12,8},{16,12},{20,16},{24,20},{28,24},{32,28}... | collective-permute-start | bytes 165896 | tf_op jit(solution)/shard_map/ppermute | solution.py:29
  29.4 7.3 %slice-start = ((bf16[4,48,576]{2,1,0:T(8,128)(2,1)}), bf16[3,48,576]{2,1,0:T(8,128)(2,1)S(1)}, s32[]{:S(2)}) async-start(bf16[4,48,576]{2,1,0:T(8,128)(2,1)} %param.9), calls=%async_computation.2 | async-start | bytes 368640 | tf_op jit(solution)/shard_map/slice | solution.py:104
  37.8 23.1 %all-to-all-start.1 = ((bf16[4,4,48,576]{3,2,1,0:T(8,128)(2,1)}), bf16[4,4,48,576]{3,2,1,0:T(8,128)(2,1)S(1)}, u32[]{:S(2)}, u32[]{:S(2)}) async-start(bf16[4,4,48,576]{3,2,1,0:T(8,128)(2,1)} %broadcast_in_dim.176), calls=%async_computation.1 | async-start | bytes 1966080 | tf_op jit(solution)/shard_map/all_to_all | solution.py:13
  43.7 4.9 %copy-start = (bf16[4,48,6,96]{3,1,2,0:T(8,128)(2,1)S(1)}, bf16[4,48,6,96]{3,1,2,0:T(8,128)(2,1)}, u32[]{:S(2)}) copy-start(bf16[4,48,6,96]{3,1,2,0:T(8,128)(2,1)} %get-tuple-element.7) | copy-start | bytes 663556
  43.7 4.9 %copy-start.1 = (bf16[4,48,6,96]{3,1,2,0:T(8,128)(2,1)S(1)}, bf16[4,48,6,96]{3,1,2,0:T(8,128)(2,1)}, u32[]{:S(2)}) copy-start(bf16[4,48,6,96]{3,1,2,0:T(8,128)(2,1)} %get-tuple-element.8) | copy-start | bytes 663556
  48.5 1.1 %copy-start.3 = (f32[4,48,6,6]{3,1,2,0:T(8,128)S(1)}, f32[4,48,6,6]{3,1,2,0:T(8,128)}, u32[]{:S(2)}) copy-start(f32[4,48,6,6]{3,1,2,0:T(8,128)} %subtract_convert_fusion) | copy-start | bytes 82948
  48.5 1.1 %copy-start.4 = (bf16[4,48,6,6]{3,1,2,0:T(8,128)(2,1)S(1)}, bf16[4,48,6,6]{3,1,2,0:T(8,128)(2,1)}, u32[]{:S(2)}) copy-start(bf16[4,48,6,6]{3,1,2,0:T(8,128)(2,1)} %get-tuple-element.9) | copy-start | bytes 41476
  48.5 1.2 %copy-start.5 = (bf16[4,48,6,6]{3,1,2,0:T(8,128)(2,1)S(1)}, bf16[4,48,6,6]{3,1,2,0:T(8,128)(2,1)}, u32[]{:S(2)}) copy-start(bf16[4,48,6,6]{3,1,2,0:T(8,128)(2,1)} %get-tuple-element.10) | copy-start | bytes 41476
  48.5 1.3 %copy-start.8 = (bf16[4,6,6,6,6,1]{4,0,3,2,1,5:T(4,128)(2,1)S(1)}, bf16[4,6,6,6,6,1]{4,0,3,2,1,5:T(4,128)(2,1)}, u32[]{:S(2)}) copy-start(bf16[4,6,6,6,6,1]{4,0,3,2,1,5:T(4,128)(2,1)} %fusion.36) | copy-start | bytes 31108
where the time goes:
time: 73.1 us; the launch traced here: 71.8 us
  starting transfers between devices  30.8 us (42%)
  other arithmetic  21.1 us (29%)
  matrix products  11 us (15%)
  local copies, waits for them, and re-layouts  8.69 us (12%)
    ppermute x1, starting transfers between devices, passed_along(): lax.ppermute(x, axis, [(i, (i + by) % length) for i in range(length)])  21.7 us
    mul x2, other arithmetic, per_device(): piece.reshape(col_dev, count_rows, D, BLOCK)  9.55 us
    all_to_all x2, starting transfers between devices, from_everyone(): lax.all_to_all(jnp.broadcast_to(x[None], (length, *x.shape)), axis, 0, 0,...  9.11 us
    dot_general x1, matrix products, per_device(): jnp.einsum('cplub,cludr->cpdrb', absorbed, row_m, preferred_element_type=...  6.61 us
    concatenate x1, other arithmetic, per_device(): jnp.concatenate([mixed * (block_par == 0).astype(jnp.bfloat16)[..., None]...  4.49 us
    dot_general x1, matrix products, per_device(): jnp.einsum('cpdrb,cbre->cpde', mixed_dense, piece_m, preferred_element_ty...  3.73 us
    broadcast_in_dim x2, local copies, waits for them, and re-layouts, from_everyone(): jnp.broadcast_to(x[None], (length, *x.shape))  3.12 us
    another operation x2, local copies, waits for them, and re-layouts, per_device(): piece.reshape(col_dev, count_rows, D, BLOCK)  2.45 us
  transfers between devices with their start and end apart: 3, of which 0 were waited for; matrix products, arithmetic and copies ran while one was open for 36% of the time, Pallas kernels for 0%

commit v1 on v0

v1 whole, which is shorter than its diff:
```python
import functools

import jax
import jax.numpy as jnp
from jax import lax
from jax.experimental import pallas as pl
from jax.experimental.pallas import tpu as pltpu
from jax.sharding import PartitionSpec as P

CHI = 128
BLOCK = 96
D = 6
LANES = 128
SUB = 8
PAIRS = D * D
KRON = PAIRS * SUB
META = 4 * D + 4
SHIFTS = (2, 1, 3)

BF16 = jnp.bfloat16
F32 = jnp.float32


def passed_along(x, axis, by):
    length = lax.axis_size(axis)
    return lax.ppermute(x, axis, [(i, (i + by) % length) for i in range(length)])


def limit_of(count, parity):
    return jnp.where(parity == 0, count, CHI - count)


def scalars(meta_ref, col):
    def leg(kind, i):
        return meta_ref[col * META + kind * D + i]

    charge = [meta_ref[col * META + 4 * D + i] for i in range(4)]
    return leg, charge


def by_six(index, values):
    out = jnp.full(index.shape, values[0], jnp.int32)
    for i in range(1, D):
        out = jnp.where(index == i, values[i], out)
    return out


def prep_kernel(meta_ref, blk_ref, left_ref, row_ref, dense_ref, kron_ref):
    cols, sub_rows, _ = left_ref.shape
    parity = blk_ref[0] * sub_rows // BLOCK
    dense_ref[...] = jnp.zeros_like(dense_ref)
    spread = (
        lax.broadcasted_iota(jnp.int32, (KRON, PAIRS), 0) // SUB
        == lax.broadcasted_iota(jnp.int32, (KRON, PAIRS), 1)
    ).astype(F32).astype(BF16)
    diag = (
        lax.broadcasted_iota(jnp.int32, (KRON, KRON), 0) % SUB
        == lax.broadcasted_iota(jnp.int32, (KRON, KRON), 1) % SUB
    )
    pair_row = lax.broadcasted_iota(jnp.int32, (PAIRS, 1), 0)
    pair_col = lax.broadcasted_iota(jnp.int32, (1, PAIRS), 1)

    def one(col, carry):
        leg, _ = scalars(meta_ref, col)
        for l in range(D):
            piece = left_ref[col, :, l * BLOCK : (l + 1) * BLOCK]
            sel = (parity + leg(0, l)) % 2
            start = pl.multiple_of(sel * LANES, LANES)
            dense_ref[col, l * sub_rows : (l + 1) * sub_rows, pl.ds(start, LANES)] = jnp.concatenate(
                [piece, jnp.zeros((sub_rows, LANES - BLOCK), BF16)], axis=1
            )
        left_leg = by_six(pair_row // D, [leg(0, i) for i in range(D)])
        up_leg = by_six(pair_row % D, [leg(1, i) for i in range(D)])
        down_leg = by_six(pair_col // D, [leg(2, i) for i in range(D)])
        right_leg = by_six(pair_col % D, [leg(3, i) for i in range(D)])
        keep = (left_leg + up_leg + down_leg + right_leg) % 2 == 0
        block_par = (parity + down_leg + right_leg) % 2
        sign = (1 - 2 * left_leg * up_leg) * (1 - 2 * block_par * down_leg)
        row = row_ref[col].astype(F32) * jnp.where(keep, sign, 0).astype(F32)
        half = lax.dot_general(
            spread, row.astype(BF16), (((1,), (1,)), ((), ())), preferred_element_type=F32
        )
        full = lax.dot_general(
            half.astype(BF16), spread, (((1,), (1,)), ((), ())), preferred_element_type=F32
        )
        kron_ref[col] = jnp.where(diag, full, 0.0).astype(BF16)
        return carry

    lax.fori_loop(0, cols, one, 0)


def absorb_kernel(meta_ref, blk_ref, *refs):
    pieces, (dense_ref, kron_ref, mixed_ref, bound, total, split) = refs[:4], refs[4:]
    cols, sub_rows, _ = pieces[0].shape
    blk = blk_ref[0]
    groups = sub_rows // (2 * SUB)
    bound[...] = jnp.zeros_like(bound)
    row_at = lax.broadcasted_iota(jnp.int32, (sub_rows, BLOCK), 0)
    col_at = lax.broadcasted_iota(jnp.int32, (sub_rows, BLOCK), 1)

    def one(col, carry):
        leg, (in_here, _, in_next, _) = scalars(meta_ref, col)
        for piece, shift in zip(pieces, (0,) + SHIFTS):
            first = (blk + 4 - shift) % 4 * sub_rows
            parity = first // BLOCK
            place = first % BLOCK
            rows_live = row_at < limit_of(in_here, parity) - place
            start = pl.multiple_of(parity * LANES + place, 2 * SUB)
            for u in range(D):
                sel = (parity + leg(1, u)) % 2
                live = rows_live & (col_at < limit_of(in_next, sel))
                mask = jnp.where(live, 1.0, 0.0).astype(BF16)
                part = piece[col, :, u * BLOCK : (u + 1) * BLOCK] * mask
                bound[pl.ds(start, sub_rows), u * LANES : u * LANES + BLOCK] = part
        total[...] = jnp.dot(dense_ref[col], bound[...], preferred_element_type=F32)
        for l in range(D):
            for group in range(groups):
                for side in range(2):
                    at = l * sub_rows + (2 * group + side) * SUB
                    for u in range(0, D, 2):
                        both = jnp.concatenate(
                            [
                                total[at : at + SUB, u * LANES : (u + 1) * LANES],
                                total[at : at + SUB, (u + 1) * LANES : (u + 2) * LANES],
                            ],
                            axis=0,
                        )
                        to = (l * D + u) * SUB
                        split[group, to : to + 2 * SUB, side * LANES : (side + 1) * LANES] = both.astype(BF16)
        for group in range(groups):
            out = jnp.dot(kron_ref[col], split[group], preferred_element_type=F32)
            for d in range(D):
                for r in range(D):
                    at = (d * D + r) * SUB
                    both = jnp.concatenate(
                        [out[at : at + SUB, :LANES], out[at : at + SUB, LANES:]], axis=0
                    )
                    to = d * sub_rows + group * 2 * SUB
                    mixed_ref[col, to : to + 2 * SUB, r * LANES : (r + 1) * LANES] = both.astype(BF16)
        return carry

    lax.fori_loop(0, cols, one, 0)


def close_kernel(meta_ref, blk_ref, *refs):
    pieces, (mixed_ref, out_ref, right) = refs[:4], refs[4:]
    cols, sub_rows, _ = pieces[0].shape
    blk = blk_ref[0]
    own = blk * sub_rows
    own_parity = own // BLOCK
    own_place = own % BLOCK
    right[...] = jnp.zeros_like(right)
    row_at = lax.broadcasted_iota(jnp.int32, (sub_rows, BLOCK), 0)
    col_at = lax.broadcasted_iota(jnp.int32, (sub_rows, BLOCK), 1)

    def one(col, carry):
        leg, (_, out_here, _, out_next) = scalars(meta_ref, col)
        for piece, shift in zip(pieces, (0,) + SHIFTS):
            first = (blk + 4 - shift) % 4 * sub_rows
            parity = first // BLOCK
            place = first % BLOCK
            for r in range(D):
                sel = (parity + leg(3, r)) % 2
                start = pl.multiple_of(r * LANES + place, 2 * SUB)
                right[sel, pl.ds(start, sub_rows), :BLOCK] = piece[col, :, r * BLOCK : (r + 1) * BLOCK]
        both = jnp.concatenate([right[0], right[1]], axis=1)
        out = jnp.dot(mixed_ref[col], both, preferred_element_type=F32)
        rows_live = row_at < limit_of(out_here, own_parity) - own_place
        for d in range(D):
            sel = (own_parity + leg(2, d)) % 2
            rows = out[d * sub_rows : (d + 1) * sub_rows]
            picked = jnp.where(sel == 0, rows[:, :BLOCK], rows[:, LANES : LANES + BLOCK])
            live = rows_live & (col_at < limit_of(out_next, sel))
            out_ref[col, :, d * BLOCK : (d + 1) * BLOCK] = jnp.where(live, picked, 0.0).astype(BF16)
        return carry

    lax.fori_loop(0, cols, one, 0)


SMEM = pl.BlockSpec(memory_space=pltpu.SMEM)
VMEM = pl.BlockSpec(memory_space=pltpu.VMEM)


def per_device(boundary, row_tensor, left_proj, right_proj, leg_parity, bond_charges):
    cols, sub_rows, merged = boundary.shape
    bonds = leg_parity.shape[0]
    start_col = lax.axis_index("col") * cols
    after = lax.rem(start_col + cols, bonds)
    legs = jnp.concatenate(
        [
            lax.dynamic_slice_in_dim(leg_parity, start_col, cols, 0),
            lax.dynamic_slice_in_dim(leg_parity, after, 1, 0),
        ],
        axis=0,
    )
    charges = jnp.concatenate(
        [
            lax.dynamic_slice_in_dim(bond_charges, start_col, cols, 0),
            lax.dynamic_slice_in_dim(bond_charges, after, 1, 0),
        ],
        axis=0,
    )
    meta = jnp.concatenate(
        [legs[:cols].reshape(cols, 3 * D), legs[1:, 0], charges[:cols], charges[1:]], axis=1
    ).reshape(cols * META)
    blk = lax.axis_index("blk").astype(jnp.int32).reshape(1)

    bound_pieces = [boundary] + [passed_along(boundary, "blk", s) for s in SHIFTS]
    halo = passed_along(right_proj[:1], "col", -1)
    right_next = jnp.concatenate([right_proj[1:], halo], axis=0)
    right_pieces = [right_next] + [passed_along(right_next, "blk", s) for s in SHIFTS]

    dense, kron = pl.pallas_call(
        prep_kernel,
        out_shape=(
            jax.ShapeDtypeStruct((cols, D * sub_rows, 2 * LANES), BF16),
            jax.ShapeDtypeStruct((cols, KRON, KRON), BF16),
        ),
        in_specs=[SMEM, SMEM, VMEM, VMEM],
        out_specs=(VMEM, VMEM),
        cost_estimate=pl.CostEstimate(flops=10**8, bytes_accessed=10**6, transcendentals=0),
        name="prep",
    )(meta, blk, left_proj, row_tensor.reshape(cols, PAIRS, PAIRS))

    mixed = pl.pallas_call(
        absorb_kernel,
        out_shape=jax.ShapeDtypeStruct((cols, D * sub_rows, D * LANES), BF16),
        in_specs=[SMEM, SMEM] + [VMEM] * 6,
        out_specs=VMEM,
        scratch_shapes=[
            pltpu.VMEM((2 * LANES, D * LANES), BF16),
            pltpu.VMEM((D * sub_rows, D * LANES), F32),
            pltpu.VMEM((sub_rows // (2 * SUB), KRON, 2 * LANES), BF16),
        ],
        cost_estimate=pl.CostEstimate(flops=10**9, bytes_accessed=4 * 10**6, transcendentals=0),
        name="absorb",
    )(meta, blk, *bound_pieces, dense, kron)

    return pl.pallas_call(
        close_kernel,
        out_shape=jax.ShapeDtypeStruct((cols, sub_rows, merged), BF16),
        in_specs=[SMEM, SMEM] + [VMEM] * 5,
        out_specs=VMEM,
        scratch_shapes=[pltpu.VMEM((2, D * LANES, LANES), BF16)],
        cost_estimate=pl.CostEstimate(flops=10**9, bytes_accessed=3 * 10**6, transcendentals=0),
        name="close",
    )(meta, blk, *right_pieces, mixed)


def solution(mesh):
    in_specs = (
        P(("grp", "col"), "blk", None),
        P(("grp", "col"), None, None, None, None),
        P(("grp", "col"), "blk", None),
        P(("grp", "col"), "blk", None),
        P("grp", None, None),
        P("grp", None),
    )
    out_specs = P(("grp", "col"), "blk", None)
    return jax.shard_map(
        per_device, mesh=mesh, in_specs=in_specs, out_specs=out_specs, check_vma=False
    )
```

time: 73.1 us -> 56.3 us (0.77); the launches traced: 71.8 us -> 56 us
  other arithmetic: 21.1 us -> 0.2 us
  Pallas kernels: 0 us -> 16.1 us
  matrix products: 11 us -> 0 us
    pallas_call x0 -> x3, Pallas kernels: none -> 16.1 us  [the longest x1 7.67 us: per_device(): pl.pallas_call(absorb_kernel, out_shape=jax.ShapeDtypeStruct((cols, D * s...]
    mul x6 -> x0, other arithmetic: 12.2 us -> none  [the longest x2 9.55 us: per_device(): piece.reshape(col_dev, count_rows, D, BLOCK)]
    dot_general x3 -> x0, matrix products: 11 us -> none  [the longest x1 6.61 us: per_device(): jnp.einsum('cplub,cludr->cpdrb', absorbed, row_m, preferred_element_type=...]
    ppermute x1 -> x7, starting transfers between devices: 21.7 us -> 31.1 us  [passed_along(): lax.ppermute(x, axis, [(i, (i + by) % length) for i in range(length)])]
    all_to_all x2 -> x0, starting transfers between devices: 9.11 us -> none  [from_everyone(): lax.all_to_all(jnp.broadcast_to(x[None], (length, *x.shape)), axis, 0, 0,...]
    concatenate x3 -> x4, other arithmetic: 4.6 us -> 0.2 us  [the longest x1 0.08 us: per_device(): jnp.concatenate([legs[:cols].reshape(cols, 3 * D), legs[1:, 0], charges[:...]
    broadcast_in_dim x2 -> x0, local copies, waits for them, and re-layouts: 3.12 us -> none  [from_everyone(): jnp.broadcast_to(x[None], (length, *x.shape))]
    convert_element_type x3 -> x0, other arithmetic: 2.52 us -> none  [the longest x1 1.24 us: per_device(): (block_par == 0).astype(jnp.bfloat16)[..., None]]
  transfers between devices with their start and end apart: 3 -> 7, of which waited for: 0 -> 0; matrix products, arithmetic and copies ran while one was open for 36% -> 12% of each run, Pallas kernels for 0% -> 20%
where the time goes in v1:
time: 56.3 us; the launch traced here: 56 us
  starting transfers between devices  31.1 us (55%)
  Pallas kernels  16.1 us (29%)
  local copies, waits for them, and re-layouts  8.5 us (15%)
    ppermute x7, starting transfers between devices, passed_along(): lax.ppermute(x, axis, [(i, (i + by) % length) for i in range(length)])  31.1 us
    pallas_call x1, Pallas kernels, per_device(): pl.pallas_call(absorb_kernel, out_shape=jax.ShapeDtypeStruct((cols, D * s...  7.67 us
    pallas_call x1, Pallas kernels, per_device(): pl.pallas_call(close_kernel, out_shape=jax.ShapeDtypeStruct((cols, sub_ro...  4.79 us
    pallas_call x1, Pallas kernels, per_device(): pl.pallas_call(prep_kernel, out_shape=(jax.ShapeDtypeStruct((cols, D * su...  3.62 us
    unnamed x18, local copies, waits for them, and re-layouts  2.41 us
    reshape x2, local copies, waits for them, and re-layouts, per_device(): row_tensor.reshape(cols, PAIRS, PAIRS)  1.79 us
  transfers between devices with their start and end apart: 7, of which 0 were waited for; matrix products, arithmetic and copies ran while one was open for 12% of the time, Pallas kernels for 20%

profile of v1, /device:TPU:40, one launch (start us, length us, event | category | flops | bytes accessed | tf_op | source)
XLA Modules:
  0.0 56.0 jit_solution(254498091834639682)
XLA Ops:
  0.0 0.0 copy-start
  0.0 3.3 %collective-permute-start.4 = (bf16[4,48,576]{2,1,0:T(8,128)(2,1)}, bf16[4,48,576]{2,1,0:T(8,128)(2,1)S(1)}, u32[]{:S(2)}, u32[]{:S(2)}) collective-permute-start(bf16[4,48,576]{2,1,0:T(8,128)(2,1)} %refs_0_.1), channel_id=1, source_target_pairs={{0,2},{1,3},{2,0},{3,1},{4,6},{5,7},{6,4},{7,5},{8,10},{9,11},{10,... | collective-permute-start | bytes 663560 | tf_op jit(solution)/shard_map/ppermute | solution.py:26
  3.3 0.7 %collective-permute-start.5 = (bf16[4,48,576]{2,1,0:T(8,128)(2,1)}, bf16[4,48,576]{2,1,0:T(8,128)(2,1)S(1)}, u32[]{:S(2)}, u32[]{:S(2)}) collective-permute-start(bf16[4,48,576]{2,1,0:T(8,128)(2,1)} %refs_0_.1), channel_id=1, source_target_pairs={{0,1},{1,2},{2,3},{3,0},{4,5},{5,6},{6,7},{7,4},{8,9},{9,10},{10,1... | collective-permute-start | bytes 663560 | tf_op jit(solution)/shard_map/ppermute | solution.py:26
  4.0 2.5 %collective-permute-start.6 = (bf16[4,48,576]{2,1,0:T(8,128)(2,1)}, bf16[4,48,576]{2,1,0:T(8,128)(2,1)S(1)}, u32[]{:S(2)}, u32[]{:S(2)}) collective-permute-start(bf16[4,48,576]{2,1,0:T(8,128)(2,1)} %refs_0_.1), channel_id=1, source_target_pairs={{0,3},{1,0},{2,1},{3,2},{4,7},{5,4},{6,5},{7,6},{8,11},{9,8},{10,9... | collective-permute-start | bytes 663560 | tf_op jit(solution)/shard_map/ppermute | solution.py:26
  6.5 0.8 %slice.15 = bf16[1,48,576]{2,1,0:T(8,128)(2,1)S(1)} slice(bf16[4,48,576]{2,1,0:T(8,128)(2,1)} %param.9), slice={[0:1], [0:48], [0:576]} | slice | bytes 110592 | tf_op jit(solution)/shard_map/slice | solution.py:209
  7.4 21.0 %collective-permute-start = (bf16[1,48,576]{2,1,0:T(8,128)(2,1)S(1)}, bf16[1,48,576]{2,1,0:T(8,128)(2,1)S(1)}, u32[]{:S(2)}, u32[]{:S(2)}) collective-permute-start(bf16[1,48,576]{2,1,0:T(8,128)(2,1)S(1)} %slice.15), channel_id=1, source_target_pairs={{0,124},{4,0},{8,4},{12,8},{16,12},{20,16},{24,20},{28,24},{32,28}... | collective-permute-start | bytes 165896 | tf_op jit(solution)/shard_map/ppermute | solution.py:26
  28.4 0.0 copy-done
  28.4 0.1 constant_dynamic-slice_fusion.2
  28.5 0.1 constant_dynamic-slice_fusion.3
  28.6 0.8 %constant_dynamic-slice_fusion = s32[1,2]{0,1:T(2,128)S(1)} fusion(s32[128,2]{0,1:T(2,128)} %param.11, s32[]{:T(128)S(6)} %select_n.9), kind=kLoop, calls=%fused_computation.4 | loop fusion | bytes 20 | tf_op jit(solution)/shard_map/dynamic_slice | solution.py:199
  29.3 0.1 pad_add_fusion
  29.4 0.8 %constant_dynamic-slice_fusion.1 = s32[4,2]{0,1:T(2,128)S(1)} fusion(s32[128,2]{0,1:T(2,128)} %param.11, s32[]{:T(128)S(6)} %select_n.8), kind=kLoop, calls=%fused_computation.5 | loop fusion | bytes 68 | tf_op jit(solution)/shard_map/dynamic_slice | solution.py:198
  30.1 0.9 %slice.14 = bf16[3,48,576]{2,1,0:T(8,128)(2,1)S(1)} slice(bf16[4,48,576]{2,1,0:T(8,128)(2,1)} %param.9), slice={[1:4], [0:48], [0:576]} | slice | bytes 331776 | tf_op jit(solution)/shard_map/slice | solution.py:210
  31.1 0.1 copy.34
  31.2 0.1 copy.33
  31.3 0.0 collective-permute-done
  31.3 0.0 copy-start.4
  31.3 0.1 collective-permute-start.1
  31.5 1.1 %collective-permute-start.2 = (bf16[4,48,576]{2,1,0:T(8,128)(2,1)S(1)}, bf16[4,48,576]{2,1,0:T(8,128)(2,1)S(1)}, u32[]{:S(2)}, u32[]{:S(2)}) collective-permute-start(bf16[4,48,576]{2,1,0:T(8,128)(2,1)S(1)} %pad_maximum_fusion.refs_0_), channel_id=1, source_target_pairs={{0,1},{1,2},{2,3},{3,0},{4,5},{5,6},{6,7},{7,4},{8,9},{9,10},{10,1... | collective-permute-start | bytes 663560 | tf_op jit(solution)/shard_map/ppermute | solution.py:26
  32.6 0.0 collective-permute-done.4.refs_1_
  32.6 0.0 copy-start.1
  32.6 2.2 %collective-permute-start.3 = (bf16[4,48,576]{2,1,0:T(8,128)(2,1)S(1)}, bf16[4,48,576]{2,1,0:T(8,128)(2,1)S(1)}, u32[]{:S(2)}, u32[]{:S(2)}) collective-permute-start(bf16[4,48,576]{2,1,0:T(8,128)(2,1)S(1)} %pad_maximum_fusion.refs_0_), channel_id=1, source_target_pairs={{0,3},{1,0},{2,1},{3,2},{4,7},{5,4},{6,5},{7,6},{8,11},{9,8},{10,9... | collective-permute-start | bytes 663560 | tf_op jit(solution)/shard_map/ppermute | solution.py:26
  34.8 0.1 copy.25
  35.0 0.1 copy.26
  35.0 0.1 reshape.12
  35.1 0.1 pad_add_fusion.2
  35.2 0.6 %reshape.13.meta_ref = s32[112]{0:T(128)} reshape(s32[4,28]{1,0:T(4,128)S(1)} %pad_add_fusion.2) | data formatting | bytes 896 | tf_op jit(solution)/shard_map/reshape | solution.py:205
  35.8 1.0 %copy.31 = bf16[4,6,6,6,6]{4,3,2,1,0:T(8,128)(2,1)S(1)} copy(bf16[4,6,6,6,6]{4,0,3,2,1:T(4,128)(2,1)} %param.7) | data formatting | bytes 20736 | tf_op jit(solution)/shard_map/reshape | solution.py:223
  36.8 0.8 %reshape.16.row_ref = bf16[4,36,36]{2,1,0:T(8,128)(2,1)} reshape(bf16[4,6,6,6,6]{4,3,2,1,0:T(8,128)(2,1)S(1)} %copy.31) | data formatting | bytes 20736 | tf_op jit(solution)/shard_map/reshape | solution.py:223
  37.6 3.6 %prep.1 = (bf16[4,288,256]{2,1,0:T(8,128)(2,1)}, bf16[4,288,288]{2,1,0:T(8,128)(2,1)}) custom-call(s32[112]{0:T(128)} %reshape.13.meta_ref, s32[1]{0:T(128)} %bitcast.1.blk_ref, bf16[4,48,576]{2,1,0:T(8,128)(2,1)} %left_ref.1, bf16[4,36,36]{2,1,0:T(8,128)(2,1)} %reshape.16.row_ref), custom_call_target="tpu_custom_call" | custom-call | flops 100000000 | bytes 1000000 | tf_op jit(solution)/shard_map/prep/pallas_call | solution.py:213
  41.2 0.0 collective-permute-done.5.refs_2_
  41.2 0.0 copy-start.2
  41.2 0.0 collective-permute-done.6.refs_3_
  41.2 0.0 copy-start.3
  41.2 0.0 copy-done.1
  41.2 0.7 %copy-done.2 = bf16[4,48,576]{2,1,0:T(8,128)(2,1)} copy-done((bf16[4,48,576]{2,1,0:T(8,128)(2,1)}, bf16[4,48,576]{2,1,0:T(8,128)(2,1)S(1)}, u32[]{:S(2)}) %copy-start.2) | copy-done | bytes 221208
  41.9 0.1 copy-done.3
  42.0 7.7 %absorb.1.refs_4_ = bf16[4,288,768]{2,1,0:T(8,128)(2,1)} custom-call(s32[112]{0:T(128)} %reshape.13.meta_ref, s32[1]{0:T(128)} %bitcast.1.blk_ref, bf16[4,48,576]{2,1,0:T(8,128)(2,1)} %refs_0_.1, bf16[4,48,576]{2,1,0:T(8,128)(2,1)} %copy-done.1, bf16[4,48,576]{2,1,0:T(8,128)(2,1)} %copy-done.2, bf16[4,48,576]{2,1,0:T(8,128)(2,1)} %copy-done.3, ...), custom_call_target="tpu_custom_call" | custom-call | flops 1000000000 | bytes 4000000 | tf_op jit(solution)/shard_map/absorb/pallas_call | solution.py:225
  49.7 0.0 copy-done.4
  49.7 0.0 collective-permute-done.1.refs_1_
  49.7 0.0 copy-start.5
  49.7 0.0 collective-permute-done.2.refs_2_
  49.7 0.0 copy-start.6
  49.7 0.0 collective-permute-done.3.refs_3_
  49.7 0.7 %copy-done.5 = bf16[4,48,576]{2,1,0:T(8,128)(2,1)} copy-done((bf16[4,48,576]{2,1,0:T(8,128)(2,1)}, bf16[4,48,576]{2,1,0:T(8,128)(2,1)S(1)}, u32[]{:S(2)}) %copy-start.5) | copy-done | bytes 221208
  50.4 0.1 copy-done.6
  50.5 0.0 copy-start.7
  50.5 0.7 %copy-done.7 = bf16[4,48,576]{2,1,0:T(8,128)(2,1)} copy-done((bf16[4,48,576]{2,1,0:T(8,128)(2,1)}, bf16[4,48,576]{2,1,0:T(8,128)(2,1)S(1)}, u32[]{:S(2)}) %copy-start.7) | copy-done | bytes 221208
  51.2 4.8 %close.1 = bf16[4,48,576]{2,1,0:T(8,128)(2,1)} custom-call(s32[112]{0:T(128)} %reshape.13.meta_ref, s32[1]{0:T(128)} %bitcast.1.blk_ref, bf16[4,48,576]{2,1,0:T(8,128)(2,1)} %copy-done.4, bf16[4,48,576]{2,1,0:T(8,128)(2,1)} %copy-done.5, bf16[4,48,576]{2,1,0:T(8,128)(2,1)} %copy-done.6, bf16[4,48,576]{2,1,0:T(8,128)(2,1)} %copy-done.7, ...), custom_call_target="tpu_custom_call" | custom-call | flops 1000000000 | bytes 3000000 | tf_op jit(solution)/shard_map/close/pallas_call | solution.py:239
  (3 shorter events, 0.1 us)
Async XLA Ops:
  0.0 28.4 %copy-start = (s32[128,3,6]{0,2,1:T(8,128)S(1)}, s32[128,3,6]{0,2,1:T(8,128)}, u32[]{:S(2)}) copy-start(s32[128,3,6]{0,2,1:T(8,128)} %param.10) | copy-start | bytes 27652
  0.0 32.6 %collective-permute-start.4 = (bf16[4,48,576]{2,1,0:T(8,128)(2,1)}, bf16[4,48,576]{2,1,0:T(8,128)(2,1)S(1)}, u32[]{:S(2)}, u32[]{:S(2)}) collective-permute-start(bf16[4,48,576]{2,1,0:T(8,128)(2,1)} %refs_0_.1), channel_id=1, source_target_pairs={{0,2},{1,3},{2,0},{3,1},{4,6},{5,7},{6,4},{7,5},{8,10},{9,11},{10,... | collective-permute-start | bytes 663560 | tf_op jit(solution)/shard_map/ppermute | solution.py:26
  3.3 37.9 %collective-permute-start.5 = (bf16[4,48,576]{2,1,0:T(8,128)(2,1)}, bf16[4,48,576]{2,1,0:T(8,128)(2,1)S(1)}, u32[]{:S(2)}, u32[]{:S(2)}) collective-permute-start(bf16[4,48,576]{2,1,0:T(8,128)(2,1)} %refs_0_.1), channel_id=1, source_target_pairs={{0,1},{1,2},{2,3},{3,0},{4,5},{5,6},{6,7},{7,4},{8,9},{9,10},{10,1... | collective-permute-start | bytes 663560 | tf_op jit(solution)/shard_map/ppermute | solution.py:26
  4.0 37.2 %collective-permute-start.6 = (bf16[4,48,576]{2,1,0:T(8,128)(2,1)}, bf16[4,48,576]{2,1,0:T(8,128)(2,1)S(1)}, u32[]{:S(2)}, u32[]{:S(2)}) collective-permute-start(bf16[4,48,576]{2,1,0:T(8,128)(2,1)} %refs_0_.1), channel_id=1, source_target_pairs={{0,3},{1,0},{2,1},{3,2},{4,7},{5,4},{6,5},{7,6},{8,11},{9,8},{10,9... | collective-permute-start | bytes 663560 | tf_op jit(solution)/shard_map/ppermute | solution.py:26
  7.4 23.9 %collective-permute-start = (bf16[1,48,576]{2,1,0:T(8,128)(2,1)S(1)}, bf16[1,48,576]{2,1,0:T(8,128)(2,1)S(1)}, u32[]{:S(2)}, u32[]{:S(2)}) collective-permute-start(bf16[1,48,576]{2,1,0:T(8,128)(2,1)S(1)} %slice.15), channel_id=1, source_target_pairs={{0,124},{4,0},{8,4},{12,8},{16,12},{20,16},{24,20},{28,24},{32,28}... | collective-permute-start | bytes 165896 | tf_op jit(solution)/shard_map/ppermute | solution.py:26
  31.3 18.4 %copy-start.4 = (bf16[4,48,576]{2,1,0:T(8,128)(2,1)}, bf16[4,48,576]{2,1,0:T(8,128)(2,1)S(1)}, u32[]{:S(2)}) copy-start(bf16[4,48,576]{2,1,0:T(8,128)(2,1)S(1)} %pad_maximum_fusion.refs_0_) | copy-start | bytes 663556
  31.3 18.3 %collective-permute-start.1 = (bf16[4,48,576]{2,1,0:T(8,128)(2,1)S(1)}, bf16[4,48,576]{2,1,0:T(8,128)(2,1)S(1)}, u32[]{:S(2)}, u32[]{:S(2)}) collective-permute-start(bf16[4,48,576]{2,1,0:T(8,128)(2,1)S(1)} %pad_maximum_fusion.refs_0_), channel_id=1, source_target_pairs={{0,2},{1,3},{2,0},{3,1},{4,6},{5,7},{6,4},{7,5},{8,10},{9,11},{10,... | collective-permute-start | bytes 663560 | tf_op jit(solution)/shard_map/ppermute | solution.py:26
  31.5 18.2 %collective-permute-start.2 = (bf16[4,48,576]{2,1,0:T(8,128)(2,1)S(1)}, bf16[4,48,576]{2,1,0:T(8,128)(2,1)S(1)}, u32[]{:S(2)}, u32[]{:S(2)}) collective-permute-start(bf16[4,48,576]{2,1,0:T(8,128)(2,1)S(1)} %pad_maximum_fusion.refs_0_), channel_id=1, source_target_pairs={{0,1},{1,2},{2,3},{3,0},{4,5},{5,6},{6,7},{7,4},{8,9},{9,10},{10,1... | collective-permute-start | bytes 663560 | tf_op jit(solution)/shard_map/ppermute | solution.py:26
  32.6 8.6 %copy-start.1 = (bf16[4,48,576]{2,1,0:T(8,128)(2,1)}, bf16[4,48,576]{2,1,0:T(8,128)(2,1)S(1)}, u32[]{:S(2)}) copy-start(bf16[4,48,576]{2,1,0:T(8,128)(2,1)S(1)} %collective-permute-done.4.refs_1_) | copy-start | bytes 663556
  32.6 17.1 %collective-permute-start.3 = (bf16[4,48,576]{2,1,0:T(8,128)(2,1)S(1)}, bf16[4,48,576]{2,1,0:T(8,128)(2,1)S(1)}, u32[]{:S(2)}, u32[]{:S(2)}) collective-permute-start(bf16[4,48,576]{2,1,0:T(8,128)(2,1)S(1)} %pad_maximum_fusion.refs_0_), channel_id=1, source_target_pairs={{0,3},{1,0},{2,1},{3,2},{4,7},{5,4},{6,5},{7,6},{8,11},{9,8},{10,9... | collective-permute-start | bytes 663560 | tf_op jit(solution)/shard_map/ppermute | solution.py:26
  41.2 0.7 %copy-start.2 = (bf16[4,48,576]{2,1,0:T(8,128)(2,1)}, bf16[4,48,576]{2,1,0:T(8,128)(2,1)S(1)}, u32[]{:S(2)}) copy-start(bf16[4,48,576]{2,1,0:T(8,128)(2,1)S(1)} %collective-permute-done.5.refs_2_) | copy-start | bytes 663556
  41.2 0.8 %copy-start.3 = (bf16[4,48,576]{2,1,0:T(8,128)(2,1)}, bf16[4,48,576]{2,1,0:T(8,128)(2,1)S(1)}, u32[]{:S(2)}) copy-start(bf16[4,48,576]{2,1,0:T(8,128)(2,1)S(1)} %collective-permute-done.6.refs_3_) | copy-start | bytes 663556
  49.7 0.7 %copy-start.5 = (bf16[4,48,576]{2,1,0:T(8,128)(2,1)}, bf16[4,48,576]{2,1,0:T(8,128)(2,1)S(1)}, u32[]{:S(2)}) copy-start(bf16[4,48,576]{2,1,0:T(8,128)(2,1)S(1)} %collective-permute-done.1.refs_1_) | copy-start | bytes 663556
  49.7 0.8 %copy-start.6 = (bf16[4,48,576]{2,1,0:T(8,128)(2,1)}, bf16[4,48,576]{2,1,0:T(8,128)(2,1)S(1)}, u32[]{:S(2)}) copy-start(bf16[4,48,576]{2,1,0:T(8,128)(2,1)S(1)} %collective-permute-done.2.refs_2_) | copy-start | bytes 663556
  50.5 0.7 %copy-start.7 = (bf16[4,48,576]{2,1,0:T(8,128)(2,1)}, bf16[4,48,576]{2,1,0:T(8,128)(2,1)S(1)}, u32[]{:S(2)}) copy-start(bf16[4,48,576]{2,1,0:T(8,128)(2,1)S(1)} %collective-permute-done.3.refs_3_) | copy-start | bytes 663556

commit v2 on v1

v2 whole, which is shorter than its diff:
```python
import jax
import jax.numpy as jnp
from jax import lax
from jax.experimental import pallas as pl
from jax.experimental.pallas import tpu as pltpu
from jax.sharding import PartitionSpec as P


CHI = 128
BLOCK = 96
D = 6
LANES = 128
SUB = 8
PAIRS = D * D
KRON = PAIRS * SUB
SHIFTS = (2, 3, 1)
VMEM_LIMIT = 20 * 1024 * 1024

BF16 = jnp.bfloat16
F32 = jnp.float32


def passed_along(x, axis, by):
    length = lax.axis_size(axis)
    return lax.ppermute(x, axis, [(i, (i + by) % length) for i in range(length)])


def limit_of(count, parity):
    return jnp.where(parity == 0, count, CHI - count)


def by_six(index, values):
    out = jnp.full(index.shape, values[0], jnp.int32)
    for i in range(1, D):
        out = jnp.where(index == i, values[i], out)
    return out


def own_rows(sub_rows):
    first = lax.axis_index("blk") * sub_rows
    return first // BLOCK, first % BLOCK


def piece_rows(shift, sub_rows):
    count = lax.axis_size("blk")
    first = (lax.axis_index("blk") + count - shift) % count * sub_rows
    return first // BLOCK, first % BLOCK


class Tables:
    def __init__(self, legs_ref, charges_ref, legs, charges, sems):
        self.legs, self.charges = legs, charges
        self.copies = [
            pltpu.make_async_copy(legs_ref, legs, sems.at[0]),
            pltpu.make_async_copy(charges_ref, charges, sems.at[1]),
        ]
        self.bonds = legs.shape[2]

    def start(self):
        for copy in self.copies:
            copy.start()

    def wait(self):
        for copy in self.copies:
            copy.wait()

    def column(self, cols, col):
        here = lax.axis_index("col") * cols + col
        after = lax.rem(here + 1, self.bonds)
        legs = [[self.legs[kind, i, here] for i in range(D)] for kind in range(3)]
        legs.append([self.legs[0, i, after] for i in range(D)])
        charges = [self.charges[i, at] for at in (here, after) for i in range(2)]
        return legs, charges


def prep_kernel(
    legs_ref, charges_ref, left_ref, row_ref, dense_ref, kron_ref, live_ref, legs_s, charges_s, sems
):
    cols, sub_rows, _ = left_ref.shape
    tables = Tables(legs_ref, charges_ref, legs_s, charges_s, sems)
    tables.start()
    parity, _ = own_rows(sub_rows)
    dense_ref[...] = jnp.zeros_like(dense_ref)
    spread = (
        lax.broadcasted_iota(jnp.int32, (KRON, PAIRS), 0) // SUB
        == lax.broadcasted_iota(jnp.int32, (KRON, PAIRS), 1)
    ).astype(F32).astype(BF16)
    diag = (
        lax.broadcasted_iota(jnp.int32, (KRON, KRON), 0) % SUB
        == lax.broadcasted_iota(jnp.int32, (KRON, KRON), 1) % SUB
    )
    pair_row = lax.broadcasted_iota(jnp.int32, (PAIRS, 1), 0)
    pair_col = lax.broadcasted_iota(jnp.int32, (1, PAIRS), 1)
    lane = lax.broadcasted_iota(jnp.int32, (1, LANES), 1)
    tables.wait()

    for col in range(cols):
        legs, (in_here, _, in_next, _) = tables.column(cols, col)
        for l in range(D):
            sel = (parity + legs[0][l]) % 2
            start = pl.multiple_of(sel * LANES, LANES)
            live = jnp.where(lane < limit_of(in_here, sel), 1.0, 0.0).astype(BF16)
            piece = jnp.concatenate(
                [left_ref[col, :, l * BLOCK : (l + 1) * BLOCK], jnp.zeros((sub_rows, LANES - BLOCK), BF16)],
                axis=1,
            )
            dense_ref[col, l * sub_rows : (l + 1) * sub_rows, pl.ds(start, LANES)] = piece * live
            for u in range(0, D, 2):
                rows = [
                    jnp.broadcast_to(
                        jnp.where(lane < limit_of(in_next, (sel + legs[1][v]) % 2), 1.0, 0.0), (SUB, LANES)
                    )
                    for v in (u, u + 1)
                ]
                at = (l * D + u) * SUB
                live_ref[col, at : at + 2 * SUB] = jnp.concatenate(rows, axis=0).astype(BF16)
        left_leg = by_six(pair_row // D, legs[0])
        up_leg = by_six(pair_row % D, legs[1])
        down_leg = by_six(pair_col // D, legs[2])
        right_leg = by_six(pair_col % D, legs[3])
        keep = (left_leg + up_leg + down_leg + right_leg) % 2 == 0
        block_par = (parity + down_leg + right_leg) % 2
        sign = (1 - 2 * left_leg * up_leg) * (1 - 2 * block_par * down_leg)
        row = row_ref[col].astype(F32) * jnp.where(keep, sign, 0).astype(F32)
        half = lax.dot_general(
            spread, row.astype(BF16), (((1,), (1,)), ((), ())), preferred_element_type=F32
        )
        full = lax.dot_general(
            half.astype(BF16), spread, (((1,), (1,)), ((), ())), preferred_element_type=F32
        )
        kron_ref[col] = jnp.where(diag, full, 0.0).astype(BF16)


def absorb_kernel(*refs):
    pieces, (dense_ref, kron_ref, live_ref, mixed_ref, bound, split) = refs[:4], refs[4:]
    cols, sub_rows, _ = pieces[0].shape
    groups = sub_rows // (2 * SUB)
    gap = jnp.zeros((LANES - BLOCK, D * LANES), BF16)
    for col in range(cols):
        bound[col, BLOCK:LANES] = gap
        bound[col, LANES + BLOCK :] = gap
    pad = jnp.zeros((sub_rows, LANES - BLOCK), BF16)

    for col in range(cols):
        for piece, shift in zip(pieces, (0,) + SHIFTS):
            parity, place = piece_rows(shift, sub_rows)
            start = pl.multiple_of(parity * LANES + place, 2 * SUB)
            for u in range(D):
                part = jnp.concatenate([piece[col, :, u * BLOCK : (u + 1) * BLOCK], pad], axis=1)
                bound[col, pl.ds(start, sub_rows), u * LANES : (u + 1) * LANES] = part
        for u in range(0, D, 2):
            total = jnp.dot(
                dense_ref[col], bound[col, :, u * LANES : (u + 2) * LANES], preferred_element_type=F32
            )
            for l in range(D):
                to = (l * D + u) * SUB
                live = live_ref[col, to : to + 2 * SUB]
                for group in range(groups):
                    for side in range(2):
                        at = l * sub_rows + (2 * group + side) * SUB
                        rows = total[at : at + SUB]
                        both = jnp.concatenate([rows[:, :LANES], rows[:, LANES:]], axis=0).astype(BF16)
                        split[col, group, to : to + 2 * SUB, side * LANES : (side + 1) * LANES] = both * live
        for group in range(groups):
            out = jnp.dot(kron_ref[col], split[col, group], preferred_element_type=F32)
            for d in range(D):
                for r in range(D):
                    at = (d * D + r) * SUB
                    rows = out[at : at + SUB]
                    both = jnp.concatenate([rows[:, :LANES], rows[:, LANES:]], axis=0).astype(BF16)
                    to = d * sub_rows + group * 2 * SUB
                    mixed_ref[col, to : to + 2 * SUB, r * LANES : (r + 1) * LANES] = both


def close_kernel(legs_ref, charges_ref, *refs):
    pieces, (mixed_ref, out_ref, right, legs_s, charges_s, sems) = refs[:4], refs[4:]
    cols, sub_rows, _ = pieces[0].shape
    tables = Tables(legs_ref, charges_ref, legs_s, charges_s, sems)
    tables.start()
    own_parity, own_place = own_rows(sub_rows)
    gap = jnp.zeros((LANES - BLOCK, LANES), BF16)
    pad = jnp.zeros((sub_rows, LANES - BLOCK), BF16)
    row_at = lax.broadcasted_iota(jnp.int32, (sub_rows, BLOCK), 0)
    col_at = lax.broadcasted_iota(jnp.int32, (sub_rows, BLOCK), 1)
    for col in range(cols):
        for r in range(D):
            for q in range(2):
                right[col, q, r, BLOCK:] = gap
        for piece, shift in zip(pieces, (0,) + SHIFTS):
            parity, place = piece_rows(shift, sub_rows)
            start = pl.multiple_of(place, 2 * SUB)
            for r in range(D):
                part = jnp.concatenate([piece[col, :, r * BLOCK : (r + 1) * BLOCK], pad], axis=1)
                right[col, parity, r, pl.ds(start, sub_rows)] = part
    tables.wait()
    for col in range(cols):
        legs, (_, out_here, _, out_next) = tables.column(cols, col)
        out = None
        for r in range(0, D, 2):
            both = jnp.concatenate(
                [
                    jnp.concatenate([right[col, legs[3][v], v], right[col, 1 - legs[3][v], v]], axis=1)
                    for v in (r, r + 1)
                ],
                axis=0,
            )
            term = jnp.dot(mixed_ref[col, :, r * LANES : (r + 2) * LANES], both, preferred_element_type=F32)
            out = term if out is None else out + term
        rows_live = row_at < limit_of(out_here, own_parity) - own_place
        for d in range(D):
            sel = (own_parity + legs[2][d]) % 2
            rows = out[d * sub_rows : (d + 1) * sub_rows]
            picked = jnp.where(sel == 0, rows[:, :BLOCK], rows[:, LANES : LANES + BLOCK])
            live = rows_live & (col_at < limit_of(out_next, sel))
            out_ref[col, :, d * BLOCK : (d + 1) * BLOCK] = jnp.where(live, picked, 0.0).astype(BF16)


def token_kernel(token_ref):
    token_ref[...] = jnp.zeros_like(token_ref)


def head_kernel(token_ref, right_ref, head_ref):
    head_ref[...] = right_ref[:1]


def join_kernel(right_ref, halo_ref, next_ref):
    cols = right_ref.shape[0]
    next_ref[: cols - 1] = right_ref[1:]
    next_ref[cols - 1 :] = halo_ref[...]


VMEM = pl.BlockSpec(memory_space=pltpu.VMEM)


def local(kernel, out_shape, operands, scratch=(), flops=0, limit=VMEM_LIMIT, space=pltpu.VMEM):
    leaves = jax.tree.leaves(out_shape)
    moved = sum(x.size * x.dtype.itemsize for x in [*operands, *leaves])
    return pl.pallas_call(
        kernel,
        out_shape=out_shape,
        in_specs=[pl.BlockSpec(memory_space=space)] * len(operands),
        out_specs=jax.tree.map(lambda _: VMEM, out_shape),
        scratch_shapes=list(scratch),
        cost_estimate=pl.CostEstimate(flops=flops, bytes_accessed=moved, transcendentals=0),
        compiler_params=pltpu.CompilerParams(vmem_limit_bytes=limit),
    )(*operands)


def per_device(boundary, row_tensor, left_proj, right_proj, leg_parity, bond_charges):
    cols, sub_rows, merged = boundary.shape
    legs = leg_parity.transpose(1, 2, 0)
    charges = bond_charges.T
    shape = jax.ShapeDtypeStruct
    tables = [
        pltpu.SMEM(legs.shape, jnp.int32),
        pltpu.SMEM(charges.shape, jnp.int32),
        pltpu.SemaphoreType.DMA((2,)),
    ]
    small = 2 * 1024 * 1024

    token = local(token_kernel, shape((SUB, LANES), F32), [], flops=4 * 10**9, limit=small)
    head = local(head_kernel, shape((1, sub_rows, merged), BF16), [token, right_proj], flops=4 * 10**9, limit=small)
    halo = passed_along(head, "col", -1)
    bound_pieces = [boundary]
    for s in SHIFTS:
        bound_pieces.append(passed_along(boundary, "blk", s))
    right_next = local(join_kernel, shape(right_proj.shape, BF16), [right_proj, halo], flops=4 * 10**9, limit=small)
    right_pieces = [right_next]
    for s in SHIFTS:
        right_pieces.append(passed_along(right_next, "blk", s))

    dense, kron, live = local(
        prep_kernel,
        (
            shape((cols, D * sub_rows, 2 * LANES), BF16),
            shape((cols, KRON, KRON), BF16),
            shape((cols, KRON, LANES), BF16),
        ),
        [legs, charges, left_proj, row_tensor.reshape(cols, PAIRS, PAIRS)],
        tables,
        flops=10**8,
    )
    mixed = local(
        absorb_kernel,
        shape((cols, D * sub_rows, D * LANES), BF16),
        [*bound_pieces, dense, kron, live],
        [
            pltpu.VMEM((cols, 2 * LANES, D * LANES), BF16),
            pltpu.VMEM((cols, sub_rows // (2 * SUB), KRON, 2 * LANES), BF16),
        ],
        flops=10**9,
    )
    return local(
        close_kernel,
        shape((cols, sub_rows, merged), BF16),
        [legs, charges, *right_pieces, mixed],
        [pltpu.VMEM((cols, 2, D, LANES, LANES), BF16), *tables],
        flops=10**9,
    )


def solution(mesh):
    in_specs = (
        P(("grp", "col"), "blk", None),
        P(("grp", "col"), None, None, None, None),
        P(("grp", "col"), "blk", None),
        P(("grp", "col"), "blk", None),
        P("grp", None, None),
        P("grp", None),
    )
    out_specs = P(("grp", "col"), "blk", None)
    return jax.shard_map(per_device, mesh=mesh, in_specs=in_specs, out_specs=out_specs, check_vma=False)
```

time: 56.3 us -> 45.7 us (0.81)
  the two profiles are of different devices: /device:TPU:40 before, /device:TPU:33 now
where the time goes in v2:
time: 45.7 us; the launch traced here: 45.6 us
  starting transfers between devices  25.6 us (56%)
  waiting for transfers between devices  11.8 us (26%)
  Pallas kernels  6.84 us (15%)
  local copies, waits for them, and re-layouts  1.21 us (3%)
    ppermute x7, starting transfers between devices, passed_along(): lax.ppermute(x, axis, [(i, (i + by) % length) for i in range(length)])  25.6 us
    ppermute x7, waiting for transfers between devices, passed_along(): lax.ppermute(x, axis, [(i, (i + by) % length) for i in range(length)])  11.8 us
    pallas_call x6, Pallas kernels, local(): pl.pallas_call(kernel, out_shape=out_shape, in_specs=[pl.BlockSpec(memory...  6.84 us
    unnamed x12, local copies, waits for them, and re-layouts  0.97 us
  transfers between devices with their start and end apart: 7, of which 4 were waited for; matrix products, arithmetic and copies ran while one was open for 1% of the time, Pallas kernels for 10%

profile of v2, /device:TPU:33, one launch (start us, length us, event | category | flops | bytes accessed | tf_op | source)
XLA Modules:
  0.0 45.6 jit_solution(15019405825003333392)
XLA Ops:
  0.0 0.0 copy-start.1
  0.0 0.9 %copy-done.1 = bf16[4,48,576]{2,1,0:T(8,128)(2,1)S(1)} copy-done((bf16[4,48,576]{2,1,0:T(8,128)(2,1)S(1)}, bf16[4,48,576]{2,1,0:T(8,128)(2,1)}, u32[]{:S(2)}) %copy-start.1) | copy-done | bytes 221208
  0.9 0.0 copy-start
  1.0 0.0 copy-start.5
  1.0 0.0 copy-start.2
  1.0 0.0 copy-start.3
  1.0 0.0 copy-start.4
  1.0 20.5 %collective-permute-start = (bf16[1,48,576]{2,1,0:T(8,128)(2,1)S(1)}, bf16[1,48,576]{2,1,0:T(8,128)(2,1)S(1)}, u32[]{:S(2)}, u32[]{:S(2)}) collective-permute-start(bf16[1,48,576]{2,1,0:T(8,128)(2,1)S(1)} %shard_map.65), channel_id=1, source_target_pairs={{0,124},{4,0},{8,4},{12,8},{16,12},{20,16},{24,20},{28,24},{32,28}... | collective-permute-start | bytes 165896 | tf_op jit(solution)/shard_map/ppermute | solution.py:25
  21.5 0.0 copy-done
  21.5 0.0 collective-permute-start.4
  21.5 0.0 collective-permute-start.5
  21.5 1.5 %collective-permute-start.6 = (bf16[4,48,576]{2,1,0:T(8,128)(2,1)S(1)}, bf16[4,48,576]{2,1,0:T(8,128)(2,1)S(1)}, u32[]{:S(2)}, u32[]{:S(2)}) collective-permute-start(bf16[4,48,576]{2,1,0:T(8,128)(2,1)S(1)} %copy-done), channel_id=1, source_target_pairs={{0,1},{1,2},{2,3},{3,0},{4,5},{5,6},{6,7},{7,4},{8,9},{9,10},{10,1... | collective-permute-start | bytes 663560 | tf_op jit(solution)/shard_map/ppermute | solution.py:25
  22.9 0.0 collective-permute-done.halo_ref
  23.0 3.1 %collective-permute-start.1 = (bf16[4,48,576]{2,1,0:T(8,128)(2,1)S(1)}, bf16[4,48,576]{2,1,0:T(8,128)(2,1)S(1)}, u32[]{:S(2)}, u32[]{:S(2)}) collective-permute-start(bf16[4,48,576]{2,1,0:T(8,128)(2,1)S(1)} %shard_map.66.refs_0_), channel_id=1, source_target_pairs={{0,2},{1,3},{2,0},{3,1},{4,6},{5,7},{6,4},{7,5},{8,10},{9,11},{10,... | collective-permute-start | bytes 663560 | tf_op jit(solution)/shard_map/ppermute | solution.py:25
  26.1 0.6 %collective-permute-start.2 = (bf16[4,48,576]{2,1,0:T(8,128)(2,1)S(1)}, bf16[4,48,576]{2,1,0:T(8,128)(2,1)S(1)}, u32[]{:S(2)}, u32[]{:S(2)}) collective-permute-start(bf16[4,48,576]{2,1,0:T(8,128)(2,1)S(1)} %shard_map.66.refs_0_), channel_id=1, source_target_pairs={{0,3},{1,0},{2,1},{3,2},{4,7},{5,4},{6,5},{7,6},{8,11},{9,8},{10,9... | collective-permute-start | bytes 663560 | tf_op jit(solution)/shard_map/ppermute | solution.py:25
  26.7 1.5 %collective-permute-done.4.refs_1_ = bf16[4,48,576]{2,1,0:T(8,128)(2,1)S(1)} collective-permute-done((bf16[4,48,576]{2,1,0:T(8,128)(2,1)S(1)}, bf16[4,48,576]{2,1,0:T(8,128)(2,1)S(1)}, u32[]{:S(2)}, u32[]{:S(2)}) %collective-permute-start.4) | collective-permute-done | bytes 221216 | tf_op jit(solution)/shard_map/ppermute | solution.py:25
  28.1 0.0 collective-permute-start.3
  28.1 0.0 copy-done.5
  28.1 0.1 copy.10
  28.2 0.2 reshape.4.row_ref
  28.4 0.0 copy-done.2
  28.4 0.0 copy-done.3
  28.4 0.0 copy-done.4
  28.4 1.9 %shard_map.67 = (bf16[4,288,256]{2,1,0:T(8,128)(2,1)S(1)}, bf16[4,288,288]{2,1,0:T(8,128)(2,1)S(1)}, bf16[4,288,128]{2,1,0:T(8,128)(2,1)S(1)}) custom-call(s32[3,6,128]{2,1,0:T(8,128)S(1)} %bitcast.2, s32[2,128]{1,0:T(2,128)S(1)} %bitcast.4, bf16[4,48,576]{2,1,0:T(8,128)(2,1)S(1)} %copy-done.2, bf16[4,36,36]{2,1,0:T(8,128)(2,1)S(1)} %reshape.4.row_ref), custom_call_target="tpu_custom_call" | custom-call | flops 100000000 | bytes 1790080 | tf_op jit(solution)/shard_map/pallas_call | solution.py:238
  30.4 0.0 collective-permute-done.5.refs_2_
  30.4 2.5 %collective-permute-done.6.refs_3_ = bf16[4,48,576]{2,1,0:T(8,128)(2,1)S(1)} collective-permute-done((bf16[4,48,576]{2,1,0:T(8,128)(2,1)S(1)}, bf16[4,48,576]{2,1,0:T(8,128)(2,1)S(1)}, u32[]{:S(2)}, u32[]{:S(2)}) %collective-permute-start.6) | collective-permute-done | bytes 221216 | tf_op jit(solution)/shard_map/ppermute | solution.py:25
  32.9 2.6 %shard_map.68.refs_4_ = bf16[4,288,768]{2,1,0:T(8,128)(2,1)S(1)} custom-call(bf16[4,48,576]{2,1,0:T(8,128)(2,1)S(1)} %copy-done, bf16[4,48,576]{2,1,0:T(8,128)(2,1)S(1)} %collective-permute-done.4.refs_1_, bf16[4,48,576]{2,1,0:T(8,128)(2,1)S(1)} %collective-permute-done.5.refs_2_, bf16[4,48,576]{2,1,0:T(8,128)(2,1)S(1)} %collective-permute-done.6.refs_3_, ...), custom_call_target="tpu_custom_call" | custom-call | flops 1000000000 | bytes 4202496 | tf_op jit(solution)/shard_map/pallas_call | solution.py:238
  35.4 2.5 %collective-permute-done.1.refs_1_ = bf16[4,48,576]{2,1,0:T(8,128)(2,1)S(1)} collective-permute-done((bf16[4,48,576]{2,1,0:T(8,128)(2,1)S(1)}, bf16[4,48,576]{2,1,0:T(8,128)(2,1)S(1)}, u32[]{:S(2)}, u32[]{:S(2)}) %collective-permute-start.1) | collective-permute-done | bytes 221216 | tf_op jit(solution)/shard_map/ppermute | solution.py:25
  37.9 0.0 collective-permute-done.2.refs_2_
  37.9 5.4 %collective-permute-done.3.refs_3_ = bf16[4,48,576]{2,1,0:T(8,128)(2,1)S(1)} collective-permute-done((bf16[4,48,576]{2,1,0:T(8,128)(2,1)S(1)}, bf16[4,48,576]{2,1,0:T(8,128)(2,1)S(1)}, u32[]{:S(2)}, u32[]{:S(2)}) %collective-permute-start.3) | collective-permute-done | bytes 221216 | tf_op jit(solution)/shard_map/ppermute | solution.py:25
  43.3 2.3 %shard_map.69 = bf16[4,48,576]{2,1,0:T(8,128)(2,1)} custom-call(s32[3,6,128]{2,1,0:T(8,128)S(1)} %bitcast.3, s32[2,128]{1,0:T(2,128)S(1)} %bitcast.5, bf16[4,48,576]{2,1,0:T(8,128)(2,1)S(1)} %shard_map.66.refs_0_, bf16[4,48,576]{2,1,0:T(8,128)(2,1)S(1)} %collective-permute-done.1.refs_1_, bf16[4,48,576]{2,1,0:T(8,128)(2,1)S(1)} %collective-permute-done.2.refs_2_, ...), custom_call_target="tpu_custom_call" | custom-call | flops 1000000000 | bytes 2885632 | tf_op jit(solution)/shard_map/pallas_call | solution.py:238
  (3 shorter events, 0.0 us)
Async XLA Ops:
  0.0 0.9 %copy-start.1 = (bf16[4,48,576]{2,1,0:T(8,128)(2,1)S(1)}, bf16[4,48,576]{2,1,0:T(8,128)(2,1)}, u32[]{:S(2)}) copy-start(bf16[4,48,576]{2,1,0:T(8,128)(2,1)} %right_ref.3) | copy-start | bytes 663556
  0.9 20.5 %copy-start = (bf16[4,48,576]{2,1,0:T(8,128)(2,1)S(1)}, bf16[4,48,576]{2,1,0:T(8,128)(2,1)}, u32[]{:S(2)}) copy-start(bf16[4,48,576]{2,1,0:T(8,128)(2,1)} %refs_0_.1) | copy-start | bytes 663556
  1.0 27.2 %copy-start.5 = (bf16[4,6,6,6,6]{4,0,3,2,1:T(4,128)(2,1)S(1)}, bf16[4,6,6,6,6]{4,0,3,2,1:T(4,128)(2,1)}, u32[]{:S(2)}) copy-start(bf16[4,6,6,6,6]{4,0,3,2,1:T(4,128)(2,1)} %param.7) | copy-start | bytes 31108
  1.0 27.4 %copy-start.2 = (bf16[4,48,576]{2,1,0:T(8,128)(2,1)S(1)}, bf16[4,48,576]{2,1,0:T(8,128)(2,1)}, u32[]{:S(2)}) copy-start(bf16[4,48,576]{2,1,0:T(8,128)(2,1)} %left_ref.1) | copy-start | bytes 663556
  1.0 27.4 %copy-start.3 = (s32[128,3,6]{0,2,1:T(8,128)S(1)}, s32[128,3,6]{0,2,1:T(8,128)}, u32[]{:S(2)}) copy-start(s32[128,3,6]{0,2,1:T(8,128)} %param.10) | copy-start | bytes 27652
  1.0 27.4 %copy-start.4 = (s32[128,2]{0,1:T(2,128)S(1)}, s32[128,2]{0,1:T(2,128)}, u32[]{:S(2)}) copy-start(s32[128,2]{0,1:T(2,128)} %param.11) | copy-start | bytes 3076
  1.0 21.9 %collective-permute-start = (bf16[1,48,576]{2,1,0:T(8,128)(2,1)S(1)}, bf16[1,48,576]{2,1,0:T(8,128)(2,1)S(1)}, u32[]{:S(2)}, u32[]{:S(2)}) collective-permute-start(bf16[1,48,576]{2,1,0:T(8,128)(2,1)S(1)} %shard_map.65), channel_id=1, source_target_pairs={{0,124},{4,0},{8,4},{12,8},{16,12},{20,16},{24,20},{28,24},{32,28}... | collective-permute-start | bytes 165896 | tf_op jit(solution)/shard_map/ppermute | solution.py:25
  21.5 6.7 %collective-permute-start.4 = (bf16[4,48,576]{2,1,0:T(8,128)(2,1)S(1)}, bf16[4,48,576]{2,1,0:T(8,128)(2,1)S(1)}, u32[]{:S(2)}, u32[]{:S(2)}) collective-permute-start(bf16[4,48,576]{2,1,0:T(8,128)(2,1)S(1)} %copy-done), channel_id=1, source_target_pairs={{0,2},{1,3},{2,0},{3,1},{4,6},{5,7},{6,4},{7,5},{8,10},{9,11},{10,... | collective-permute-start | bytes 663560 | tf_op jit(solution)/shard_map/ppermute | solution.py:25
  21.5 8.9 %collective-permute-start.5 = (bf16[4,48,576]{2,1,0:T(8,128)(2,1)S(1)}, bf16[4,48,576]{2,1,0:T(8,128)(2,1)S(1)}, u32[]{:S(2)}, u32[]{:S(2)}) collective-permute-start(bf16[4,48,576]{2,1,0:T(8,128)(2,1)S(1)} %copy-done), channel_id=1, source_target_pairs={{0,3},{1,0},{2,1},{3,2},{4,7},{5,4},{6,5},{7,6},{8,11},{9,8},{10,9... | collective-permute-start | bytes 663560 | tf_op jit(solution)/shard_map/ppermute | solution.py:25
  21.5 11.4 %collective-permute-start.6 = (bf16[4,48,576]{2,1,0:T(8,128)(2,1)S(1)}, bf16[4,48,576]{2,1,0:T(8,128)(2,1)S(1)}, u32[]{:S(2)}, u32[]{:S(2)}) collective-permute-start(bf16[4,48,576]{2,1,0:T(8,128)(2,1)S(1)} %copy-done), channel_id=1, source_target_pairs={{0,1},{1,2},{2,3},{3,0},{4,5},{5,6},{6,7},{7,4},{8,9},{9,10},{10,1... | collective-permute-start | bytes 663560 | tf_op jit(solution)/shard_map/ppermute | solution.py:25
  23.0 14.9 %collective-permute-start.1 = (bf16[4,48,576]{2,1,0:T(8,128)(2,1)S(1)}, bf16[4,48,576]{2,1,0:T(8,128)(2,1)S(1)}, u32[]{:S(2)}, u32[]{:S(2)}) collective-permute-start(bf16[4,48,576]{2,1,0:T(8,128)(2,1)S(1)} %shard_map.66.refs_0_), channel_id=1, source_target_pairs={{0,2},{1,3},{2,0},{3,1},{4,6},{5,7},{6,4},{7,5},{8,10},{9,11},{10,... | collective-permute-start | bytes 663560 | tf_op jit(solution)/shard_map/ppermute | solution.py:25
  26.1 11.9 %collective-permute-start.2 = (bf16[4,48,576]{2,1,0:T(8,128)(2,1)S(1)}, bf16[4,48,576]{2,1,0:T(8,128)(2,1)S(1)}, u32[]{:S(2)}, u32[]{:S(2)}) collective-permute-start(bf16[4,48,576]{2,1,0:T(8,128)(2,1)S(1)} %shard_map.66.refs_0_), channel_id=1, source_target_pairs={{0,3},{1,0},{2,1},{3,2},{4,7},{5,4},{6,5},{7,6},{8,11},{9,8},{10,9... | collective-permute-start | bytes 663560 | tf_op jit(solution)/shard_map/ppermute | solution.py:25
  28.1 15.2 %collective-permute-start.3 = (bf16[4,48,576]{2,1,0:T(8,128)(2,1)S(1)}, bf16[4,48,576]{2,1,0:T(8,128)(2,1)S(1)}, u32[]{:S(2)}, u32[]{:S(2)}) collective-permute-start(bf16[4,48,576]{2,1,0:T(8,128)(2,1)S(1)} %shard_map.66.refs_0_), channel_id=1, source_target_pairs={{0,1},{1,2},{2,3},{3,0},{4,5},{5,6},{6,7},{7,4},{8,9},{9,10},{10,1... | collective-permute-start | bytes 663560 | tf_op jit(solution)/shard_map/ppermute | solution.py:25

commit v3 on v2

--- a/solution.py
+++ b/solution.py
@@ -23,6 +23,10 @@
 def passed_along(x, axis, by):
     length = lax.axis_size(axis)
     return lax.ppermute(x, axis, [(i, (i + by) % length) for i in range(length)])
+
+
+def sent(x, by):
+    return passed_along(x, "blk", by)
 
 
 def limit_of(count, parity):
@@ -173,8 +177,9 @@
 
 
 def close_kernel(legs_ref, charges_ref, *refs):
-    pieces, (mixed_ref, out_ref, right, legs_s, charges_s, sems) = refs[:4], refs[4:]
-    cols, sub_rows, _ = pieces[0].shape
+    own, far, far_last, *near = refs[:5]
+    mixed_ref, out_ref, right, legs_s, charges_s, sems = refs[5:]
+    cols, sub_rows, _ = own.shape
     tables = Tables(legs_ref, charges_ref, legs_s, charges_s, sems)
     tables.start()
     own_parity, own_place = own_rows(sub_rows)
@@ -186,11 +191,13 @@
         for r in range(D):
             for q in range(2):
                 right[col, q, r, BLOCK:] = gap
-        for piece, shift in zip(pieces, (0,) + SHIFTS):
+        second = (far, col) if col < cols - 1 else (far_last, 0)
+        pieces = [(own, col), second, *((piece, col) for piece in near)]
+        for (piece, at), shift in zip(pieces, (0,) + SHIFTS):
             parity, place = piece_rows(shift, sub_rows)
             start = pl.multiple_of(place, 2 * SUB)
             for r in range(D):
-                part = jnp.concatenate([piece[col, :, r * BLOCK : (r + 1) * BLOCK], pad], axis=1)
+                part = jnp.concatenate([piece[at, :, r * BLOCK : (r + 1) * BLOCK], pad], axis=1)
                 right[col, parity, r, pl.ds(start, sub_rows)] = part
     tables.wait()
     for col in range(cols):
@@ -219,8 +226,9 @@
     token_ref[...] = jnp.zeros_like(token_ref)
 
 
-def head_kernel(token_ref, right_ref, head_ref):
+def split_kernel(token_ref, right_ref, head_ref, tail_ref):
     head_ref[...] = right_ref[:1]
+    tail_ref[...] = right_ref[1:]
 
 
 def join_kernel(right_ref, halo_ref, next_ref):
@@ -259,15 +267,19 @@
     small = 2 * 1024 * 1024
 
     token = local(token_kernel, shape((SUB, LANES), F32), [], flops=4 * 10**9, limit=small)
-    head = local(head_kernel, shape((1, sub_rows, merged), BF16), [token, right_proj], flops=4 * 10**9, limit=small)
+    head, tail = local(
+        split_kernel,
+        (shape((1, sub_rows, merged), BF16), shape((cols - 1, sub_rows, merged), BF16)),
+        [token, right_proj],
+        flops=4 * 10**9,
+        limit=small,
+    )
     halo = passed_along(head, "col", -1)
-    bound_pieces = [boundary]
-    for s in SHIFTS:
-        bound_pieces.append(passed_along(boundary, "blk", s))
+    bound_pieces = [boundary] + [sent(boundary, s) for s in SHIFTS]
     right_next = local(join_kernel, shape(right_proj.shape, BF16), [right_proj, halo], flops=4 * 10**9, limit=small)
-    right_pieces = [right_next]
-    for s in SHIFTS:
-        right_pieces.append(passed_along(right_next, "blk", s))
+    far, *near = SHIFTS
+    right_pieces = [right_next, sent(tail, far), sent(halo, far)]
+    right_pieces += [sent(right_next, s) for s in near]
 
     dense, kron, live = local(
         prep_kernel,

time: 45.7 us -> 46.2 us (1.011)
  the two profiles are of different devices: /device:TPU:33 before, /device:TPU:34 now
where the time goes in v3:
time: 46.2 us; the launch traced here: 46.1 us
  starting transfers between devices  32.1 us (69%)
  Pallas kernels  6.87 us (15%)
  waiting for transfers between devices  5.78 us (13%)
  local copies, waits for them, and re-layouts  1.21 us (3%)
    ppermute x8, starting transfers between devices, passed_along(): lax.ppermute(x, axis, [(i, (i + by) % length) for i in range(length)])  32.1 us
    pallas_call x6, Pallas kernels, local(): pl.pallas_call(kernel, out_shape=out_shape, in_specs=[pl.BlockSpec(memory...  6.87 us
    ppermute x8, waiting for transfers between devices, passed_along(): lax.ppermute(x, axis, [(i, (i + by) % length) for i in range(length)])  5.78 us
    unnamed x12, local copies, waits for them, and re-layouts  0.97 us
  transfers between devices with their start and end apart: 8, of which 2 were waited for; matrix products, arithmetic and copies ran while one was open for 1% of the time, Pallas kernels for 10%

profile of v3, /device:TPU:34, one launch (start us, length us, event | category | flops | bytes accessed | tf_op | source)
XLA Modules:
  0.0 46.1 jit_solution(15455868124720065176)
XLA Ops:
  0.0 0.0 copy-start.1
  0.0 0.9 %copy-done.1 = bf16[4,48,576]{2,1,0:T(8,128)(2,1)S(1)} copy-done((bf16[4,48,576]{2,1,0:T(8,128)(2,1)S(1)}, bf16[4,48,576]{2,1,0:T(8,128)(2,1)}, u32[]{:S(2)}) %copy-start.1) | copy-done | bytes 221208
  0.9 0.0 copy-start
  1.0 0.0 copy-start.5
  1.0 0.0 copy-start.2
  1.0 0.0 copy-start.3
  1.0 0.0 copy-start.4
  1.0 21.9 %collective-permute-start = (bf16[1,48,576]{2,1,0:T(8,128)(2,1)S(1)}, bf16[1,48,576]{2,1,0:T(8,128)(2,1)S(1)}, u32[]{:S(2)}, u32[]{:S(2)}) collective-permute-start(bf16[1,48,576]{2,1,0:T(8,128)(2,1)S(1)} %get-tuple-element.10), channel_id=1, source_target_pairs={{0,124},{4,0},{8,4},{12,8},{16,12},{20,16},{24,20},{28,24},{32,28}... | collective-permute-start | bytes 165896 | tf_op jit(solution)/shard_map/ppermute | solution.py:25
  23.0 0.0 copy-done
  23.0 2.4 %collective-permute-start.5 = (bf16[4,48,576]{2,1,0:T(8,128)(2,1)S(1)}, bf16[4,48,576]{2,1,0:T(8,128)(2,1)S(1)}, u32[]{:S(2)}, u32[]{:S(2)}) collective-permute-start(bf16[4,48,576]{2,1,0:T(8,128)(2,1)S(1)} %copy-done), channel_id=1, source_target_pairs={{0,2},{1,3},{2,0},{3,1},{4,6},{5,7},{6,4},{7,5},{8,10},{9,11},{10,... | collective-permute-start | bytes 663560 | tf_op jit(solution)/shard_map/ppermute | solution.py:25
  25.4 1.3 %collective-permute-start.6 = (bf16[4,48,576]{2,1,0:T(8,128)(2,1)S(1)}, bf16[4,48,576]{2,1,0:T(8,128)(2,1)S(1)}, u32[]{:S(2)}, u32[]{:S(2)}) collective-permute-start(bf16[4,48,576]{2,1,0:T(8,128)(2,1)S(1)} %copy-done), channel_id=1, source_target_pairs={{0,3},{1,0},{2,1},{3,2},{4,7},{5,4},{6,5},{7,6},{8,11},{9,8},{10,9... | collective-permute-start | bytes 663560 | tf_op jit(solution)/shard_map/ppermute | solution.py:25
  26.7 0.7 %collective-permute-start.7 = (bf16[4,48,576]{2,1,0:T(8,128)(2,1)S(1)}, bf16[4,48,576]{2,1,0:T(8,128)(2,1)S(1)}, u32[]{:S(2)}, u32[]{:S(2)}) collective-permute-start(bf16[4,48,576]{2,1,0:T(8,128)(2,1)S(1)} %copy-done), channel_id=1, source_target_pairs={{0,1},{1,2},{2,3},{3,0},{4,5},{5,6},{6,7},{7,4},{8,9},{9,10},{10,1... | collective-permute-start | bytes 663560 | tf_op jit(solution)/shard_map/ppermute | solution.py:25
  27.4 0.0 collective-permute-done.halo_ref
  27.4 1.4 %collective-permute-start.3 = (bf16[4,48,576]{2,1,0:T(8,128)(2,1)S(1)}, bf16[4,48,576]{2,1,0:T(8,128)(2,1)S(1)}, u32[]{:S(2)}, u32[]{:S(2)}) collective-permute-start(bf16[4,48,576]{2,1,0:T(8,128)(2,1)S(1)} %shard_map.66.refs_0_), channel_id=1, source_target_pairs={{0,3},{1,0},{2,1},{3,2},{4,7},{5,4},{6,5},{7,6},{8,11},{9,8},{10,9... | collective-permute-start | bytes 663560 | tf_op jit(solution)/shard_map/ppermute | solution.py:25
  28.8 0.7 %collective-permute-start.4 = (bf16[4,48,576]{2,1,0:T(8,128)(2,1)S(1)}, bf16[4,48,576]{2,1,0:T(8,128)(2,1)S(1)}, u32[]{:S(2)}, u32[]{:S(2)}) collective-permute-start(bf16[4,48,576]{2,1,0:T(8,128)(2,1)S(1)} %shard_map.66.refs_0_), channel_id=1, source_target_pairs={{0,1},{1,2},{2,3},{3,0},{4,5},{5,6},{6,7},{7,4},{8,9},{9,10},{10,1... | collective-permute-start | bytes 663560 | tf_op jit(solution)/shard_map/ppermute | solution.py:25
  29.5 3.8 %collective-permute-done.5.refs_1_ = bf16[4,48,576]{2,1,0:T(8,128)(2,1)S(1)} collective-permute-done((bf16[4,48,576]{2,1,0:T(8,128)(2,1)S(1)}, bf16[4,48,576]{2,1,0:T(8,128)(2,1)S(1)}, u32[]{:S(2)}, u32[]{:S(2)}) %collective-permute-start.5) | collective-permute-done | bytes 221216 | tf_op jit(solution)/shard_map/ppermute | solution.py:25
  33.4 2.3 %collective-permute-start.1 = (bf16[3,48,576]{2,1,0:T(8,128)(2,1)S(1)}, bf16[3,48,576]{2,1,0:T(8,128)(2,1)S(1)}, u32[]{:S(2)}, u32[]{:S(2)}) collective-permute-start(bf16[3,48,576]{2,1,0:T(8,128)(2,1)S(1)} %get-tuple-element.11), channel_id=1, source_target_pairs={{0,2},{1,3},{2,0},{3,1},{4,6},{5,7},{6,4},{7,5},{8,10},{9,11},{10,... | collective-permute-start | bytes 497672 | tf_op jit(solution)/shard_map/ppermute | solution.py:25
  35.7 0.0 copy-done.5
  35.7 0.1 copy.10
  35.8 0.2 reshape.4.row_ref
  35.9 0.0 copy-done.2
  36.0 0.0 copy-done.3
  36.0 0.0 copy-done.4
  36.0 2.0 %shard_map.67 = (bf16[4,288,256]{2,1,0:T(8,128)(2,1)S(1)}, bf16[4,288,288]{2,1,0:T(8,128)(2,1)S(1)}, bf16[4,288,128]{2,1,0:T(8,128)(2,1)S(1)}) custom-call(s32[3,6,128]{2,1,0:T(8,128)S(1)} %bitcast.2, s32[2,128]{1,0:T(2,128)S(1)} %bitcast.4, bf16[4,48,576]{2,1,0:T(8,128)(2,1)S(1)} %copy-done.2, bf16[4,36,36]{2,1,0:T(8,128)(2,1)S(1)} %reshape.4.row_ref), custom_call_target="tpu_custom_call" | custom-call | flops 100000000 | bytes 1790080 | tf_op jit(solution)/shard_map/pallas_call | solution.py:246
  37.9 0.0 collective-permute-done.6.refs_2_
  38.0 1.3 %collective-permute-start.2 = (bf16[1,48,576]{2,1,0:T(8,128)(2,1)S(1)}, bf16[1,48,576]{2,1,0:T(8,128)(2,1)S(1)}, u32[]{:S(2)}, u32[]{:S(2)}) collective-permute-start(bf16[1,48,576]{2,1,0:T(8,128)(2,1)S(1)} %collective-permute-done.halo_ref), channel_id=1, source_target_pairs={{0,2},{1,3},{2,0},{3,1},{4,6},{5,7},{6,4},{7,5},{8,10},{9,11},{10,... | collective-permute-start | bytes 165896 | tf_op jit(solution)/shard_map/ppermute | solution.py:25
  39.3 0.0 collective-permute-done.7.refs_3_
  39.3 2.6 %shard_map.68.refs_5_ = bf16[4,288,768]{2,1,0:T(8,128)(2,1)S(1)} custom-call(bf16[4,48,576]{2,1,0:T(8,128)(2,1)S(1)} %copy-done, bf16[4,48,576]{2,1,0:T(8,128)(2,1)S(1)} %collective-permute-done.5.refs_1_, bf16[4,48,576]{2,1,0:T(8,128)(2,1)S(1)} %collective-permute-done.6.refs_2_, bf16[4,48,576]{2,1,0:T(8,128)(2,1)S(1)} %collective-permute-done.7.refs_3_, ...), custom_call_target="tpu_custom_call" | custom-call | flops 1000000000 | bytes 4202496 | tf_op jit(solution)/shard_map/pallas_call | solution.py:246
  41.9 1.9 %collective-permute-done.2.refs_2_ = bf16[1,48,576]{2,1,0:T(8,128)(2,1)S(1)} collective-permute-done((bf16[1,48,576]{2,1,0:T(8,128)(2,1)S(1)}, bf16[1,48,576]{2,1,0:T(8,128)(2,1)S(1)}, u32[]{:S(2)}, u32[]{:S(2)}) %collective-permute-start.2) | collective-permute-done | bytes 55328 | tf_op jit(solution)/shard_map/ppermute | solution.py:25
  43.8 0.0 collective-permute-done.1.refs_1_
  43.8 0.0 collective-permute-done.3.refs_3_
  43.8 0.0 collective-permute-done.4.refs_4_
  43.8 2.3 %shard_map.69 = bf16[4,48,576]{2,1,0:T(8,128)(2,1)} custom-call(s32[3,6,128]{2,1,0:T(8,128)S(1)} %bitcast.3, s32[2,128]{1,0:T(2,128)S(1)} %bitcast.5, bf16[4,48,576]{2,1,0:T(8,128)(2,1)S(1)} %shard_map.66.refs_0_, bf16[3,48,576]{2,1,0:T(8,128)(2,1)S(1)} %collective-permute-done.1.refs_1_, bf16[1,48,576]{2,1,0:T(8,128)(2,1)S(1)} %collective-permute-done.2.refs_2_, ...), custom_call_target="tpu_custom_call" | custom-call | flops 1000000000 | bytes 2885632 | tf_op jit(solution)/shard_map/pallas_call | solution.py:246
  (3 shorter events, 0.0 us)
Async XLA Ops:
  0.0 0.9 %copy-start.1 = (bf16[4,48,576]{2,1,0:T(8,128)(2,1)S(1)}, bf16[4,48,576]{2,1,0:T(8,128)(2,1)}, u32[]{:S(2)}) copy-start(bf16[4,48,576]{2,1,0:T(8,128)(2,1)} %right_ref.3) | copy-start | bytes 663556
  0.9 22.0 %copy-start = (bf16[4,48,576]{2,1,0:T(8,128)(2,1)S(1)}, bf16[4,48,576]{2,1,0:T(8,128)(2,1)}, u32[]{:S(2)}) copy-start(bf16[4,48,576]{2,1,0:T(8,128)(2,1)} %refs_0_.1) | copy-start | bytes 663556
  1.0 34.7 %copy-start.5 = (bf16[4,6,6,6,6]{4,0,3,2,1:T(4,128)(2,1)S(1)}, bf16[4,6,6,6,6]{4,0,3,2,1:T(4,128)(2,1)}, u32[]{:S(2)}) copy-start(bf16[4,6,6,6,6]{4,0,3,2,1:T(4,128)(2,1)} %param.7) | copy-start | bytes 31108
  1.0 35.0 %copy-start.2 = (bf16[4,48,576]{2,1,0:T(8,128)(2,1)S(1)}, bf16[4,48,576]{2,1,0:T(8,128)(2,1)}, u32[]{:S(2)}) copy-start(bf16[4,48,576]{2,1,0:T(8,128)(2,1)} %left_ref.1) | copy-start | bytes 663556
  1.0 35.0 %copy-start.3 = (s32[128,3,6]{0,2,1:T(8,128)S(1)}, s32[128,3,6]{0,2,1:T(8,128)}, u32[]{:S(2)}) copy-start(s32[128,3,6]{0,2,1:T(8,128)} %param.10) | copy-start | bytes 27652
  1.0 35.0 %copy-start.4 = (s32[128,2]{0,1:T(2,128)S(1)}, s32[128,2]{0,1:T(2,128)}, u32[]{:S(2)}) copy-start(s32[128,2]{0,1:T(2,128)} %param.11) | copy-start | bytes 3076
  1.0 26.4 %collective-permute-start = (bf16[1,48,576]{2,1,0:T(8,128)(2,1)S(1)}, bf16[1,48,576]{2,1,0:T(8,128)(2,1)S(1)}, u32[]{:S(2)}, u32[]{:S(2)}) collective-permute-start(bf16[1,48,576]{2,1,0:T(8,128)(2,1)S(1)} %get-tuple-element.10), channel_id=1, source_target_pairs={{0,124},{4,0},{8,4},{12,8},{16,12},{20,16},{24,20},{28,24},{32,28}... | collective-permute-start | bytes 165896 | tf_op jit(solution)/shard_map/ppermute | solution.py:25
  23.0 10.4 %collective-permute-start.5 = (bf16[4,48,576]{2,1,0:T(8,128)(2,1)S(1)}, bf16[4,48,576]{2,1,0:T(8,128)(2,1)S(1)}, u32[]{:S(2)}, u32[]{:S(2)}) collective-permute-start(bf16[4,48,576]{2,1,0:T(8,128)(2,1)S(1)} %copy-done), channel_id=1, source_target_pairs={{0,2},{1,3},{2,0},{3,1},{4,6},{5,7},{6,4},{7,5},{8,10},{9,11},{10,... | collective-permute-start | bytes 663560 | tf_op jit(solution)/shard_map/ppermute | solution.py:25
  25.4 12.6 %collective-permute-start.6 = (bf16[4,48,576]{2,1,0:T(8,128)(2,1)S(1)}, bf16[4,48,576]{2,1,0:T(8,128)(2,1)S(1)}, u32[]{:S(2)}, u32[]{:S(2)}) collective-permute-start(bf16[4,48,576]{2,1,0:T(8,128)(2,1)S(1)} %copy-done), channel_id=1, source_target_pairs={{0,3},{1,0},{2,1},{3,2},{4,7},{5,4},{6,5},{7,6},{8,11},{9,8},{10,9... | collective-permute-start | bytes 663560 | tf_op jit(solution)/shard_map/ppermute | solution.py:25
  26.7 12.6 %collective-permute-start.7 = (bf16[4,48,576]{2,1,0:T(8,128)(2,1)S(1)}, bf16[4,48,576]{2,1,0:T(8,128)(2,1)S(1)}, u32[]{:S(2)}, u32[]{:S(2)}) collective-permute-start(bf16[4,48,576]{2,1,0:T(8,128)(2,1)S(1)} %copy-done), channel_id=1, source_target_pairs={{0,1},{1,2},{2,3},{3,0},{4,5},{5,6},{6,7},{7,4},{8,9},{9,10},{10,1... | collective-permute-start | bytes 663560 | tf_op jit(solution)/shard_map/ppermute | solution.py:25
  27.4 16.4 %collective-permute-start.3 = (bf16[4,48,576]{2,1,0:T(8,128)(2,1)S(1)}, bf16[4,48,576]{2,1,0:T(8,128)(2,1)S(1)}, u32[]{:S(2)}, u32[]{:S(2)}) collective-permute-start(bf16[4,48,576]{2,1,0:T(8,128)(2,1)S(1)} %shard_map.66.refs_0_), channel_id=1, source_target_pairs={{0,3},{1,0},{2,1},{3,2},{4,7},{5,4},{6,5},{7,6},{8,11},{9,8},{10,9... | collective-permute-start | bytes 663560 | tf_op jit(solution)/shard_map/ppermute | solution.py:25
  28.8 15.0 %collective-permute-start.4 = (bf16[4,48,576]{2,1,0:T(8,128)(2,1)S(1)}, bf16[4,48,576]{2,1,0:T(8,128)(2,1)S(1)}, u32[]{:S(2)}, u32[]{:S(2)}) collective-permute-start(bf16[4,48,576]{2,1,0:T(8,128)(2,1)S(1)} %shard_map.66.refs_0_), channel_id=1, source_target_pairs={{0,1},{1,2},{2,3},{3,0},{4,5},{5,6},{6,7},{7,4},{8,9},{9,10},{10,1... | collective-permute-start | bytes 663560 | tf_op jit(solution)/shard_map/ppermute | solution.py:25
  33.4 10.4 %collective-permute-start.1 = (bf16[3,48,576]{2,1,0:T(8,128)(2,1)S(1)}, bf16[3,48,576]{2,1,0:T(8,128)(2,1)S(1)}, u32[]{:S(2)}, u32[]{:S(2)}) collective-permute-start(bf16[3,48,576]{2,1,0:T(8,128)(2,1)S(1)} %get-tuple-element.11), channel_id=1, source_target_pairs={{0,2},{1,3},{2,0},{3,1},{4,6},{5,7},{6,4},{7,5},{8,10},{9,11},{10,... | collective-permute-start | bytes 497672 | tf_op jit(solution)/shard_map/ppermute | solution.py:25
  38.0 5.8 %collective-permute-start.2 = (bf16[1,48,576]{2,1,0:T(8,128)(2,1)S(1)}, bf16[1,48,576]{2,1,0:T(8,128)(2,1)S(1)}, u32[]{:S(2)}, u32[]{:S(2)}) collective-permute-start(bf16[1,48,576]{2,1,0:T(8,128)(2,1)S(1)} %collective-permute-done.halo_ref), channel_id=1, source_target_pairs={{0,2},{1,3},{2,0},{3,1},{4,6},{5,7},{6,4},{7,5},{8,10},{9,11},{10,... | collective-permute-start | bytes 165896 | tf_op jit(solution)/shard_map/ppermute | solution.py:25

commit v4 on v3

--- a/solution.py
+++ b/solution.py
@@ -13,7 +13,9 @@
 SUB = 8
 PAIRS = D * D
 KRON = PAIRS * SUB
+WIDTH = 6
 SHIFTS = (2, 3, 1)
+RIGHT_SHIFTS = (2, 1, 3)
 VMEM_LIMIT = 20 * 1024 * 1024
 
 BF16 = jnp.bfloat16
@@ -34,8 +36,8 @@
 
 
 def by_six(index, values):
-    out = jnp.full(index.shape, values[0], jnp.int32)
-    for i in range(1, D):
+    out = jnp.zeros(index.shape, jnp.int32)
+    for i in range(D):
         out = jnp.where(index == i, values[i], out)
     return out
 
@@ -51,40 +53,38 @@
     return first // BLOCK, first % BLOCK
 
 
-class Tables:
-    def __init__(self, legs_ref, charges_ref, legs, charges, sems):
-        self.legs, self.charges = legs, charges
-        self.copies = [
-            pltpu.make_async_copy(legs_ref, legs, sems.at[0]),
-            pltpu.make_async_copy(charges_ref, charges, sems.at[1]),
-        ]
-        self.bonds = legs.shape[2]
-
-    def start(self):
-        for copy in self.copies:
-            copy.start()
-
-    def wait(self):
-        for copy in self.copies:
-            copy.wait()
-
-    def column(self, cols, col):
-        here = lax.axis_index("col") * cols + col
-        after = lax.rem(here + 1, self.bonds)
-        legs = [[self.legs[kind, i, here] for i in range(D)] for kind in range(3)]
-        legs.append([self.legs[0, i, after] for i in range(D)])
-        charges = [self.charges[i, at] for at in (here, after) for i in range(2)]
+class Table:
+    def __init__(self, table_ref, table, sem):
+        self.table = table
+        self.copy = pltpu.make_async_copy(table_ref, table, sem)
+
+    def column(self, col):
+        def at(slot, step):
+            return self.table[0, slot * WIDTH + col + step]
+
+        legs = [[at(kind * D + i, 0) for i in range(D)] for kind in range(3)]
+        legs.append([at(i, 1) for i in range(D)])
+        charges = [at(3 * D + i, step) for step in range(2) for i in range(2)]
         return legs, charges
 
 
-def prep_kernel(
-    legs_ref, charges_ref, left_ref, row_ref, dense_ref, kron_ref, live_ref, legs_s, charges_s, sems
-):
+def packed_table(legs_ref, charges_ref, cols):
+    bonds = legs_ref.shape[2]
+    here = lax.axis_index("col") * cols
+    lane = lax.broadcasted_iota(jnp.int32, (1, bonds), 1)
+    rows = [legs_ref[kind, i : i + 1] for kind in range(3) for i in range(D)]
+    rows += [charges_ref[i : i + 1] for i in range(2)]
+    table = jnp.zeros((1, bonds), jnp.int32)
+    for slot, row in enumerate(rows):
+        turned = pltpu.roll(row, lax.rem(bonds - here + slot * WIDTH, bonds), 1)
+        table = jnp.where(lane // WIDTH == slot, turned, table)
+    return table
+
+
+def prep_kernel(table_ref, left_ref, row_ref, dense_ref, kron_ref, live_ref):
     cols, sub_rows, _ = left_ref.shape
-    tables = Tables(legs_ref, charges_ref, legs_s, charges_s, sems)
-    tables.start()
     parity, _ = own_rows(sub_rows)
-    dense_ref[...] = jnp.zeros_like(dense_ref)
+    table = table_ref[...]
     spread = (
         lax.broadcasted_iota(jnp.int32, (KRON, PAIRS), 0) // SUB
         == lax.broadcasted_iota(jnp.int32, (KRON, PAIRS), 1)
@@ -96,35 +96,44 @@
     pair_row = lax.broadcasted_iota(jnp.int32, (PAIRS, 1), 0)
     pair_col = lax.broadcasted_iota(jnp.int32, (1, PAIRS), 1)
     lane = lax.broadcasted_iota(jnp.int32, (1, LANES), 1)
-    tables.wait()
-
-    for col in range(cols):
-        legs, (in_here, _, in_next, _) = tables.column(cols, col)
+    pad = jnp.zeros((sub_rows, LANES - BLOCK), BF16)
+
+    def at(slot, step):
+        return table[:, slot * WIDTH + step : slot * WIDTH + step + 1]
+
+    def below(limit):
+        return jnp.where(lane < limit, 1, 0)
+
+    for col in range(cols):
+        left_leg = [at(i, col) for i in range(D)]
+        up_leg = [at(D + i, col) for i in range(D)]
+        down_leg = [at(2 * D + i, col) for i in range(D)]
+        right_leg = [at(i, col + 1) for i in range(D)]
+        in_here = at(3 * D, col)
+        in_next = at(3 * D, col + 1)
+        here = [below(in_here), below(CHI - in_here)]
+        after = [below(in_next), below(CHI - in_next)]
         for l in range(D):
-            sel = (parity + legs[0][l]) % 2
-            start = pl.multiple_of(sel * LANES, LANES)
-            live = jnp.where(lane < limit_of(in_here, sel), 1.0, 0.0).astype(BF16)
-            piece = jnp.concatenate(
-                [left_ref[col, :, l * BLOCK : (l + 1) * BLOCK], jnp.zeros((sub_rows, LANES - BLOCK), BF16)],
-                axis=1,
-            )
-            dense_ref[col, l * sub_rows : (l + 1) * sub_rows, pl.ds(start, LANES)] = piece * live
+            sel = (parity + left_leg[l]) % 2
+            piece = jnp.concatenate([left_ref[col, :, l * BLOCK : (l + 1) * BLOCK], pad], axis=1)
+            for half in range(2):
+                live = (here[half] * (sel if half else 1 - sel)).astype(F32).astype(BF16)
+                dense_ref[col, l * sub_rows : (l + 1) * sub_rows, half * LANES : (half + 1) * LANES] = piece * live
             for u in range(0, D, 2):
-                rows = [
-                    jnp.broadcast_to(
-                        jnp.where(lane < limit_of(in_next, (sel + legs[1][v]) % 2), 1.0, 0.0), (SUB, LANES)
-                    )
-                    for v in (u, u + 1)
-                ]
-                at = (l * D + u) * SUB
-                live_ref[col, at : at + 2 * SUB] = jnp.concatenate(rows, axis=0).astype(BF16)
-        left_leg = by_six(pair_row // D, legs[0])
-        up_leg = by_six(pair_row % D, legs[1])
-        down_leg = by_six(pair_col // D, legs[2])
-        right_leg = by_six(pair_col % D, legs[3])
-        keep = (left_leg + up_leg + down_leg + right_leg) % 2 == 0
-        block_par = (parity + down_leg + right_leg) % 2
-        sign = (1 - 2 * left_leg * up_leg) * (1 - 2 * block_par * down_leg)
+                rows = []
+                for v in (u, u + 1):
+                    odd = (sel + up_leg[v]) % 2
+                    row = after[0] * (1 - odd) + after[1] * odd
+                    rows.append(jnp.broadcast_to(row.astype(F32), (SUB, LANES)))
+                to = (l * D + u) * SUB
+                live_ref[col, to : to + 2 * SUB] = jnp.concatenate(rows, axis=0).astype(BF16)
+        left_at = by_six(pair_row // D, left_leg)
+        up_at = by_six(pair_row % D, up_leg)
+        down_at = by_six(pair_col // D, down_leg)
+        right_at = by_six(pair_col % D, right_leg)
+        keep = (left_at + up_at + down_at + right_at) % 2 == 0
+        block_par = (parity + down_at + right_at) % 2
+        sign = (1 - 2 * left_at * up_at) * (1 - 2 * block_par * down_at)
         row = row_ref[col].astype(F32) * jnp.where(keep, sign, 0).astype(F32)
         half = lax.dot_general(
             spread, row.astype(BF16), (((1,), (1,)), ((), ())), preferred_element_type=F32
@@ -176,12 +185,12 @@
                     mixed_ref[col, to : to + 2 * SUB, r * LANES : (r + 1) * LANES] = both
 
 
-def close_kernel(legs_ref, charges_ref, *refs):
-    own, far, far_last, *near = refs[:5]
-    mixed_ref, out_ref, right, legs_s, charges_s, sems = refs[5:]
+def close_kernel(table_ref, *refs):
+    own, tails, lasts, across = refs[0], refs[1:3], refs[3:5], refs[5]
+    mixed_ref, out_ref, right, table_s, sem = refs[6:]
     cols, sub_rows, _ = own.shape
-    tables = Tables(legs_ref, charges_ref, legs_s, charges_s, sems)
-    tables.start()
+    table = Table(table_ref, table_s, sem)
+    table.copy.start()
     own_parity, own_place = own_rows(sub_rows)
     gap = jnp.zeros((LANES - BLOCK, LANES), BF16)
     pad = jnp.zeros((sub_rows, LANES - BLOCK), BF16)
@@ -191,17 +200,17 @@
         for r in range(D):
             for q in range(2):
                 right[col, q, r, BLOCK:] = gap
-        second = (far, col) if col < cols - 1 else (far_last, 0)
-        pieces = [(own, col), second, *((piece, col) for piece in near)]
-        for (piece, at), shift in zip(pieces, (0,) + SHIFTS):
+        near = [(piece, col) for piece in tails] if col < cols - 1 else [(piece, 0) for piece in lasts]
+        pieces = [(own, col), *near, (across, col)]
+        for (piece, at), shift in zip(pieces, (0,) + RIGHT_SHIFTS):
             parity, place = piece_rows(shift, sub_rows)
             start = pl.multiple_of(place, 2 * SUB)
             for r in range(D):
                 part = jnp.concatenate([piece[at, :, r * BLOCK : (r + 1) * BLOCK], pad], axis=1)
                 right[col, parity, r, pl.ds(start, sub_rows)] = part
-    tables.wait()
-    for col in range(cols):
-        legs, (_, out_here, _, out_next) = tables.column(cols, col)
+    table.copy.wait()
+    for col in range(cols):
+        legs, (_, out_here, _, out_next) = table.column(col)
         out = None
         for r in range(0, D, 2):
             both = jnp.concatenate(
@@ -231,8 +240,9 @@
     tail_ref[...] = right_ref[1:]
 
 
-def join_kernel(right_ref, halo_ref, next_ref):
+def join_kernel(right_ref, halo_ref, legs_ref, charges_ref, next_ref, table_ref):
     cols = right_ref.shape[0]
+    table_ref[...] = packed_table(legs_ref, charges_ref, cols)
     next_ref[: cols - 1] = right_ref[1:]
     next_ref[cols - 1 :] = halo_ref[...]
 
@@ -259,11 +269,8 @@
     legs = leg_parity.transpose(1, 2, 0)
     charges = bond_charges.T
     shape = jax.ShapeDtypeStruct
-    tables = [
-        pltpu.SMEM(legs.shape, jnp.int32),
-        pltpu.SMEM(charges.shape, jnp.int32),
-        pltpu.SemaphoreType.DMA((2,)),
-    ]
+    line = (1, legs.shape[2])
+    lookup = [pltpu.SMEM(line, jnp.int32), pltpu.SemaphoreType.DMA]
     small = 2 * 1024 * 1024
 
     token = local(token_kernel, shape((SUB, LANES), F32), [], flops=4 * 10**9, limit=small)
@@ -276,10 +283,18 @@
     )
     halo = passed_along(head, "col", -1)
     bound_pieces = [boundary] + [sent(boundary, s) for s in SHIFTS]
-    right_next = local(join_kernel, shape(right_proj.shape, BF16), [right_proj, halo], flops=4 * 10**9, limit=small)
-    far, *near = SHIFTS
-    right_pieces = [right_next, sent(tail, far), sent(halo, far)]
-    right_pieces += [sent(right_next, s) for s in near]
+    right_next, table = local(
+        join_kernel,
+        (shape(right_proj.shape, BF16), shape(line, jnp.int32)),
+        [right_proj, halo, legs, charges],
+        flops=4 * 10**9,
+        limit=small,
+    )
+    *near, far = RIGHT_SHIFTS
+    tails = [sent(tail, s) for s in near]
+    across = sent(right_next, far)
+    lasts = [sent(halo, s) for s in near]
+    right_pieces = [right_next, *tails, *lasts, across]
 
     dense, kron, live = local(
         prep_kernel,
@@ -288,8 +303,7 @@
             shape((cols, KRON, KRON), BF16),
             shape((cols, KRON, LANES), BF16),
         ),
-        [legs, charges, left_proj, row_tensor.reshape(cols, PAIRS, PAIRS)],
-        tables,
+        [table, left_proj, row_tensor.reshape(cols, PAIRS, PAIRS)],
         flops=10**8,
     )
     mixed = local(
@@ -305,8 +319,8 @@
     return local(
         close_kernel,
         shape((cols, sub_rows, merged), BF16),
-        [legs, charges, *right_pieces, mixed],
-        [pltpu.VMEM((cols, 2, D, LANES, LANES), BF16), *tables],
+        [table, *right_pieces, mixed],
+        [pltpu.VMEM((cols, 2, D, LANES, LANES), BF16), *lookup],
         flops=10**9,
     )
 

time: 46.2 us -> 47.3 us (1.024)
  the two profiles are of different devices: /device:TPU:34 before, /device:TPU:38 now
where the time goes in v4:
time: 47.3 us; the launch traced here: 47.1 us
  starting transfers between devices  35.9 us (76%)
  Pallas kernels  6.47 us (14%)
  waiting for transfers between devices  3.42 us (7%)
  local copies, waits for them, and re-layouts  1.21 us (3%)
    ppermute x9, starting transfers between devices, passed_along(): lax.ppermute(x, axis, [(i, (i + by) % length) for i in range(length)])  35.9 us
    pallas_call x6, Pallas kernels, local(): pl.pallas_call(kernel, out_shape=out_shape, in_specs=[pl.BlockSpec(memory...  6.47 us
    ppermute x9, waiting for transfers between devices, passed_along(): lax.ppermute(x, axis, [(i, (i + by) % length) for i in range(length)])  3.42 us
    unnamed x12, local copies, waits for them, and re-layouts  0.97 us
  transfers between devices with their start and end apart: 9, of which 3 were waited for; matrix products, arithmetic and copies ran while one was open for 1% of the time, Pallas kernels for 9%

profile of v4, /device:TPU:38, one launch (start us, length us, event | category | flops | bytes accessed | tf_op | source)
XLA Modules:
  0.0 47.1 jit_solution(8377310016161417871)
XLA Ops:
  0.0 0.0 copy-start.1
  0.0 0.9 %copy-done.1 = bf16[4,48,576]{2,1,0:T(8,128)(2,1)S(1)} copy-done((bf16[4,48,576]{2,1,0:T(8,128)(2,1)S(1)}, bf16[4,48,576]{2,1,0:T(8,128)(2,1)}, u32[]{:S(2)}) %copy-start.1) | copy-done | bytes 221208
  0.9 0.0 copy-start
  0.9 0.0 copy-start.3
  0.9 0.0 copy-start.4
  1.0 21.9 %collective-permute-start = (bf16[1,48,576]{2,1,0:T(8,128)(2,1)S(1)}, bf16[1,48,576]{2,1,0:T(8,128)(2,1)S(1)}, u32[]{:S(2)}, u32[]{:S(2)}) collective-permute-start(bf16[1,48,576]{2,1,0:T(8,128)(2,1)S(1)} %get-tuple-element.12), channel_id=1, source_target_pairs={{0,124},{4,0},{8,4},{12,8},{16,12},{20,16},{24,20},{28,24},{32,28}... | collective-permute-start | bytes 165896 | tf_op jit(solution)/shard_map/ppermute | solution.py:27
  22.9 0.0 copy-done
  22.9 1.1 %collective-permute-start.6 = (bf16[4,48,576]{2,1,0:T(8,128)(2,1)S(1)}, bf16[4,48,576]{2,1,0:T(8,128)(2,1)S(1)}, u32[]{:S(2)}, u32[]{:S(2)}) collective-permute-start(bf16[4,48,576]{2,1,0:T(8,128)(2,1)S(1)} %copy-done), channel_id=1, source_target_pairs={{0,2},{1,3},{2,0},{3,1},{4,6},{5,7},{6,4},{7,5},{8,10},{9,11},{10,... | collective-permute-start | bytes 663560 | tf_op jit(solution)/shard_map/ppermute | solution.py:27
  24.0 0.0 collective-permute-start.7
  24.0 3.2 %collective-permute-start.8 = (bf16[4,48,576]{2,1,0:T(8,128)(2,1)S(1)}, bf16[4,48,576]{2,1,0:T(8,128)(2,1)S(1)}, u32[]{:S(2)}, u32[]{:S(2)}) collective-permute-start(bf16[4,48,576]{2,1,0:T(8,128)(2,1)S(1)} %copy-done), channel_id=1, source_target_pairs={{0,1},{1,2},{2,3},{3,0},{4,5},{5,6},{6,7},{7,4},{8,9},{9,10},{10,1... | collective-permute-start | bytes 663560 | tf_op jit(solution)/shard_map/ppermute | solution.py:27
  27.3 0.0 collective-permute-done.halo_ref
  27.3 0.0 copy-done.3
  27.3 0.0 copy-done.4
  27.3 0.0 copy-start.5
  27.3 0.0 copy-start.2
  27.3 0.1 shard_map.66
  27.4 0.1 collective-permute-start.5
  27.6 2.5 %collective-permute-start.1 = (bf16[3,48,576]{2,1,0:T(8,128)(2,1)S(1)}, bf16[3,48,576]{2,1,0:T(8,128)(2,1)S(1)}, u32[]{:S(2)}, u32[]{:S(2)}) collective-permute-start(bf16[3,48,576]{2,1,0:T(8,128)(2,1)S(1)} %get-tuple-element.15), channel_id=1, source_target_pairs={{0,2},{1,3},{2,0},{3,1},{4,6},{5,7},{6,4},{7,5},{8,10},{9,11},{10,... | collective-permute-start | bytes 497672 | tf_op jit(solution)/shard_map/ppermute | solution.py:27
  30.0 2.6 %collective-permute-done.6.refs_1_ = bf16[4,48,576]{2,1,0:T(8,128)(2,1)S(1)} collective-permute-done((bf16[4,48,576]{2,1,0:T(8,128)(2,1)S(1)}, bf16[4,48,576]{2,1,0:T(8,128)(2,1)S(1)}, u32[]{:S(2)}, u32[]{:S(2)}) %collective-permute-start.6) | collective-permute-done | bytes 221216 | tf_op jit(solution)/shard_map/ppermute | solution.py:27
  32.6 0.7 %collective-permute-start.2 = (bf16[3,48,576]{2,1,0:T(8,128)(2,1)S(1)}, bf16[3,48,576]{2,1,0:T(8,128)(2,1)S(1)}, u32[]{:S(2)}, u32[]{:S(2)}) collective-permute-start(bf16[3,48,576]{2,1,0:T(8,128)(2,1)S(1)} %get-tuple-element.15), channel_id=1, source_target_pairs={{0,1},{1,2},{2,3},{3,0},{4,5},{5,6},{6,7},{7,4},{8,9},{9,10},{10,1... | collective-permute-start | bytes 497672 | tf_op jit(solution)/shard_map/ppermute | solution.py:27
  33.3 0.0 copy-done.5
  33.3 0.1 copy.10
  33.4 0.2 reshape.4.row_ref
  33.6 0.0 copy-done.2
  33.6 1.6 %shard_map.67 = (bf16[4,288,256]{2,1,0:T(8,128)(2,1)S(1)}, bf16[4,288,288]{2,1,0:T(8,128)(2,1)S(1)}, bf16[4,288,128]{2,1,0:T(8,128)(2,1)S(1)}) custom-call(s32[1,128]{1,0:T(1,128)S(1)} %get-tuple-element.13.table_ref, bf16[4,48,576]{2,1,0:T(8,128)(2,1)S(1)} %copy-done.2, bf16[4,36,36]{2,1,0:T(8,128)(2,1)S(1)} %reshape.4.row_ref), custom_call_target="tpu_custom_call" | custom-call | flops 100000000 | bytes 1780352 | tf_op jit(solution)/shard_map/pallas_call | solution.py:256
  35.2 0.6 %collective-permute-done.7.refs_2_ = bf16[4,48,576]{2,1,0:T(8,128)(2,1)S(1)} collective-permute-done((bf16[4,48,576]{2,1,0:T(8,128)(2,1)S(1)}, bf16[4,48,576]{2,1,0:T(8,128)(2,1)S(1)}, u32[]{:S(2)}, u32[]{:S(2)}) %collective-permute-start.7) | collective-permute-done | bytes 221216 | tf_op jit(solution)/shard_map/ppermute | solution.py:27
  35.8 2.2 %collective-permute-start.3 = (bf16[1,48,576]{2,1,0:T(8,128)(2,1)S(1)}, bf16[1,48,576]{2,1,0:T(8,128)(2,1)S(1)}, u32[]{:S(2)}, u32[]{:S(2)}) collective-permute-start(bf16[1,48,576]{2,1,0:T(8,128)(2,1)S(1)} %collective-permute-done.halo_ref), channel_id=1, source_target_pairs={{0,2},{1,3},{2,0},{3,1},{4,6},{5,7},{6,4},{7,5},{8,10},{9,11},{10,... | collective-permute-start | bytes 165896 | tf_op jit(solution)/shard_map/ppermute | solution.py:27
  38.0 0.2 collective-permute-done.8.refs_3_
  38.2 4.1 %collective-permute-start.4 = (bf16[1,48,576]{2,1,0:T(8,128)(2,1)S(1)}, bf16[1,48,576]{2,1,0:T(8,128)(2,1)S(1)}, u32[]{:S(2)}, u32[]{:S(2)}) collective-permute-start(bf16[1,48,576]{2,1,0:T(8,128)(2,1)S(1)} %collective-permute-done.halo_ref), channel_id=1, source_target_pairs={{0,1},{1,2},{2,3},{3,0},{4,5},{5,6},{6,7},{7,4},{8,9},{9,10},{10,1... | collective-permute-start | bytes 165896 | tf_op jit(solution)/shard_map/ppermute | solution.py:27
  42.4 2.6 %shard_map.68.refs_6_ = bf16[4,288,768]{2,1,0:T(8,128)(2,1)S(1)} custom-call(bf16[4,48,576]{2,1,0:T(8,128)(2,1)S(1)} %copy-done, bf16[4,48,576]{2,1,0:T(8,128)(2,1)S(1)} %collective-permute-done.6.refs_1_, bf16[4,48,576]{2,1,0:T(8,128)(2,1)S(1)} %collective-permute-done.7.refs_2_, bf16[4,48,576]{2,1,0:T(8,128)(2,1)S(1)} %collective-permute-done.8.refs_3_, ...), custom_call_target="tpu_custom_call" | custom-call | flops 1000000000 | bytes 4202496 | tf_op jit(solution)/shard_map/pallas_call | solution.py:256
  44.9 0.0 collective-permute-done.3.refs_3_
  45.0 0.0 collective-permute-done.4.refs_4_
  45.0 0.0 collective-permute-done.1.refs_1_
  45.0 0.0 collective-permute-done.2.refs_2_
  45.0 0.0 collective-permute-done.5.refs_5_
  45.0 2.1 %shard_map.69 = bf16[4,48,576]{2,1,0:T(8,128)(2,1)} custom-call(s32[1,128]{1,0:T(1,128)S(1)} %get-tuple-element.13.table_ref, bf16[4,48,576]{2,1,0:T(8,128)(2,1)S(1)} %get-tuple-element.14.refs_0_, bf16[3,48,576]{2,1,0:T(8,128)(2,1)S(1)} %collective-permute-done.1.refs_1_, bf16[3,48,576]{2,1,0:T(8,128)(2,1)S(1)} %collective-permute-done.2.refs_2_, ...), custom_call_target="tpu_custom_call" | custom-call | flops 1000000000 | bytes 2875904 | tf_op jit(solution)/shard_map/pallas_call | solution.py:256
  (2 shorter events, 0.0 us)
Async XLA Ops:
  0.0 0.9 %copy-start.1 = (bf16[4,48,576]{2,1,0:T(8,128)(2,1)S(1)}, bf16[4,48,576]{2,1,0:T(8,128)(2,1)}, u32[]{:S(2)}) copy-start(bf16[4,48,576]{2,1,0:T(8,128)(2,1)} %right_ref.3) | copy-start | bytes 663556
  0.9 22.0 %copy-start = (bf16[4,48,576]{2,1,0:T(8,128)(2,1)S(1)}, bf16[4,48,576]{2,1,0:T(8,128)(2,1)}, u32[]{:S(2)}) copy-start(bf16[4,48,576]{2,1,0:T(8,128)(2,1)} %refs_0_.1) | copy-start | bytes 663556
  0.9 26.3 %copy-start.3 = (s32[128,3,6]{0,2,1:T(8,128)S(1)}, s32[128,3,6]{0,2,1:T(8,128)}, u32[]{:S(2)}) copy-start(s32[128,3,6]{0,2,1:T(8,128)} %param.10) | copy-start | bytes 27652
  0.9 26.3 %copy-start.4 = (s32[128,2]{0,1:T(2,128)S(1)}, s32[128,2]{0,1:T(2,128)}, u32[]{:S(2)}) copy-start(s32[128,2]{0,1:T(2,128)} %param.11) | copy-start | bytes 3076
  1.0 26.3 %collective-permute-start = (bf16[1,48,576]{2,1,0:T(8,128)(2,1)S(1)}, bf16[1,48,576]{2,1,0:T(8,128)(2,1)S(1)}, u32[]{:S(2)}, u32[]{:S(2)}) collective-permute-start(bf16[1,48,576]{2,1,0:T(8,128)(2,1)S(1)} %get-tuple-element.12), channel_id=1, source_target_pairs={{0,124},{4,0},{8,4},{12,8},{16,12},{20,16},{24,20},{28,24},{32,28}... | collective-permute-start | bytes 165896 | tf_op jit(solution)/shard_map/ppermute | solution.py:27
  22.9 9.7 %collective-permute-start.6 = (bf16[4,48,576]{2,1,0:T(8,128)(2,1)S(1)}, bf16[4,48,576]{2,1,0:T(8,128)(2,1)S(1)}, u32[]{:S(2)}, u32[]{:S(2)}) collective-permute-start(bf16[4,48,576]{2,1,0:T(8,128)(2,1)S(1)} %copy-done), channel_id=1, source_target_pairs={{0,2},{1,3},{2,0},{3,1},{4,6},{5,7},{6,4},{7,5},{8,10},{9,11},{10,... | collective-permute-start | bytes 663560 | tf_op jit(solution)/shard_map/ppermute | solution.py:27
  24.0 11.7 %collective-permute-start.7 = (bf16[4,48,576]{2,1,0:T(8,128)(2,1)S(1)}, bf16[4,48,576]{2,1,0:T(8,128)(2,1)S(1)}, u32[]{:S(2)}, u32[]{:S(2)}) collective-permute-start(bf16[4,48,576]{2,1,0:T(8,128)(2,1)S(1)} %copy-done), channel_id=1, source_target_pairs={{0,3},{1,0},{2,1},{3,2},{4,7},{5,4},{6,5},{7,6},{8,11},{9,8},{10,9... | collective-permute-start | bytes 663560 | tf_op jit(solution)/shard_map/ppermute | solution.py:27
  24.0 14.2 %collective-permute-start.8 = (bf16[4,48,576]{2,1,0:T(8,128)(2,1)S(1)}, bf16[4,48,576]{2,1,0:T(8,128)(2,1)S(1)}, u32[]{:S(2)}, u32[]{:S(2)}) collective-permute-start(bf16[4,48,576]{2,1,0:T(8,128)(2,1)S(1)} %copy-done), channel_id=1, source_target_pairs={{0,1},{1,2},{2,3},{3,0},{4,5},{5,6},{6,7},{7,4},{8,9},{9,10},{10,1... | collective-permute-start | bytes 663560 | tf_op jit(solution)/shard_map/ppermute | solution.py:27
  27.3 6.0 %copy-start.5 = (bf16[4,6,6,6,6]{4,0,3,2,1:T(4,128)(2,1)S(1)}, bf16[4,6,6,6,6]{4,0,3,2,1:T(4,128)(2,1)}, u32[]{:S(2)}) copy-start(bf16[4,6,6,6,6]{4,0,3,2,1:T(4,128)(2,1)} %param.7) | copy-start | bytes 31108
  27.3 6.3 %copy-start.2 = (bf16[4,48,576]{2,1,0:T(8,128)(2,1)S(1)}, bf16[4,48,576]{2,1,0:T(8,128)(2,1)}, u32[]{:S(2)}) copy-start(bf16[4,48,576]{2,1,0:T(8,128)(2,1)} %left_ref.1) | copy-start | bytes 663556
  27.4 17.6 %collective-permute-start.5 = (bf16[4,48,576]{2,1,0:T(8,128)(2,1)S(1)}, bf16[4,48,576]{2,1,0:T(8,128)(2,1)S(1)}, u32[]{:S(2)}, u32[]{:S(2)}) collective-permute-start(bf16[4,48,576]{2,1,0:T(8,128)(2,1)S(1)} %get-tuple-element.14.refs_0_), channel_id=1, source_target_pairs={{0,3},{1,0},{2,1},{3,2},{4,7},{5,4},{6,5},{7,6},{8,11},{9,8},{10,9... | collective-permute-start | bytes 663560 | tf_op jit(solution)/shard_map/ppermute | solution.py:27
  27.6 17.4 %collective-permute-start.1 = (bf16[3,48,576]{2,1,0:T(8,128)(2,1)S(1)}, bf16[3,48,576]{2,1,0:T(8,128)(2,1)S(1)}, u32[]{:S(2)}, u32[]{:S(2)}) collective-permute-start(bf16[3,48,576]{2,1,0:T(8,128)(2,1)S(1)} %get-tuple-element.15), channel_id=1, source_target_pairs={{0,2},{1,3},{2,0},{3,1},{4,6},{5,7},{6,4},{7,5},{8,10},{9,11},{10,... | collective-permute-start | bytes 497672 | tf_op jit(solution)/shard_map/ppermute | solution.py:27
  32.6 12.4 %collective-permute-start.2 = (bf16[3,48,576]{2,1,0:T(8,128)(2,1)S(1)}, bf16[3,48,576]{2,1,0:T(8,128)(2,1)S(1)}, u32[]{:S(2)}, u32[]{:S(2)}) collective-permute-start(bf16[3,48,576]{2,1,0:T(8,128)(2,1)S(1)} %get-tuple-element.15), channel_id=1, source_target_pairs={{0,1},{1,2},{2,3},{3,0},{4,5},{5,6},{6,7},{7,4},{8,9},{9,10},{10,1... | collective-permute-start | bytes 497672 | tf_op jit(solution)/shard_map/ppermute | solution.py:27
  35.8 9.2 %collective-permute-start.3 = (bf16[1,48,576]{2,1,0:T(8,128)(2,1)S(1)}, bf16[1,48,576]{2,1,0:T(8,128)(2,1)S(1)}, u32[]{:S(2)}, u32[]{:S(2)}) collective-permute-start(bf16[1,48,576]{2,1,0:T(8,128)(2,1)S(1)} %collective-permute-done.halo_ref), channel_id=1, source_target_pairs={{0,2},{1,3},{2,0},{3,1},{4,6},{5,7},{6,4},{7,5},{8,10},{9,11},{10,... | collective-permute-start | bytes 165896 | tf_op jit(solution)/shard_map/ppermute | solution.py:27
  38.2 6.7 %collective-permute-start.4 = (bf16[1,48,576]{2,1,0:T(8,128)(2,1)S(1)}, bf16[1,48,576]{2,1,0:T(8,128)(2,1)S(1)}, u32[]{:S(2)}, u32[]{:S(2)}) collective-permute-start(bf16[1,48,576]{2,1,0:T(8,128)(2,1)S(1)} %collective-permute-done.halo_ref), channel_id=1, source_target_pairs={{0,1},{1,2},{2,3},{3,0},{4,5},{5,6},{6,7},{7,4},{8,9},{9,10},{10,1... | collective-permute-start | bytes 165896 | tf_op jit(solution)/shard_map/ppermute | solution.py:27
